TPU v7x, 256 devices: a whole 4x4x8 slice. The times are simulated.
256 devices in a mesh: seq: 16 (over z, core), head: 16 (over x, y).
Axes of the slice: x: 4, y: 4, z: 8, core: 2. Of those that a mesh axis runs over, the one named last changes fastest.
Arguments:
- queries: bfloat16 [8192, 4096], P('seq', 'head'), may hold values from -6 to 6
- keys: bfloat16 [8192, 1024], P(('seq', 'head')), may hold values from -6 to 6
- values: bfloat16 [8192, 1024], P(('seq', 'head')), may hold values from -3 to 3
- attn_out: bfloat16 [8192, 4096], P('seq', 'head'), may hold values from -1.796875 to 1.796875
- out_grad: bfloat16 [8192, 4096], P('seq', 'head'), may hold values from -6 to 6
- log_norm: float32 [32, 8192], P('head', 'seq'), may hold values from 3.5 to 5.5
- block_layout: int32 [32, 64, 64], P('head'), may hold values 0 or 1
- document_ids: int32 [8192], replicated, may hold values from 0 to 7, never falling along the last dimension, each value on 1 to 4096 neighbouring positions
- block_order: int32 [64], replicated, may hold values from 0 to 63, each once
Outputs:
- query_grad: float32 [8192, 4096], P('seq', 'head')
- key_grad: float32 [8192, 1024], P(('seq', 'head'))
- value_grad: float32 [8192, 1024], P(('seq', 'head'))
Inputs may be any that keep to these rules, and one draw needn't show every extreme that they name: `document_ids`: never falls along the sequence position; each document covers 1 to 4096 positions, one exactly 4096. `block_order`: each sequence block once.
All inputs are finite; a program needn't handle non-finite values.
Results may differ from a plain program's by a relative error of at most 0.0029.
Values may be sent and summed in bfloat16 or wider, within the bound.
No kernel may reach another device: no remote copies, remote signals or barrier semaphores. Data moves between devices by JAX's collectives and lax.ppermute only.
A program may use at most 128 MiB of HBM per device.

v0:
```python
import math

import jax
import jax.numpy as jnp
from jax import lax
from jax.experimental import pallas as pl
from jax.experimental.pallas import tpu as pltpu
from jax.sharding import Mesh, PartitionSpec as P

D = 128
BLOCK = 128
HALF = 64
CHUNK = 4 * HALF
SCALE = D ** (-0.5)
LOG2E = math.log2(math.e)
NZ = 8
NQ = 8
ROWS = 4 * BLOCK
DOCS = 8
UNROLL = 3
FIRST = (0, 4, 3, 5)
SECOND = (2, 6, 1, 7)
INS = FIRST[1:] + SECOND

HEAD = ("x", "w", "p")


def make_kernel(offsets, first):
    nc = len(offsets)
    nk = 4 * nc

    def kernel(bo, sd, code, meta, *refs):
        if first:
            q0, g0, qg1, qg2, qg3 = refs[:5]
            refs = refs[5:]
        else:
            qs, gs, dq_in = refs[:3]
            refs = refs[3:]
        a0, a1, a2, a3 = refs[:4]
        refs = refs[4:]
        kvs, refs = refs[:nc], refs[nc:]
        dqt, refs = refs[0], refs[1:]
        outs, refs = refs[:nc], refs[nc:]
        if first:
            qs, gs, refs = refs[0], refs[1], refs[2:]
        rows, spans, kv, acc, pt, dst, kvt, tags, lst, sem = refs
        z, c, p = meta[0], meta[1], meta[2]

        copies = []
        for dc in range(2):
            for dp in range(2):
                aux = ((a0, a2), (a1, a3))[dc][dp]
                for b in range(4):
                    i = dc * 4 + b
                    r = pl.ds(b * BLOCK, BLOCK)
                    for j in range(2):
                        h = dp * 2 + j
                        hr = pl.ds(h * BLOCK, BLOCK)
                        srcs = ()
                        if first and dc == 0 and dp == 0:
                            srcs = ((q0, 0, qs), (g0, 0, gs))
                        elif first:
                            sq = {(1, 0): qg1, (0, 1): qg2, (1, 1): qg3}[(dc, dp)]
                            srcs = ((sq, 0, qs), (sq, 2 * D, gs))
                        for src, o, dest in srcs:
                            cp = pltpu.make_async_copy(
                                src.at[r, pl.ds(o + j * D, D)], dest.at[i, hr, :], sem
                            )
                            cp.start()
                            copies.append(cp)
                        rs = slice(b * BLOCK, (b + 1) * BLOCK)
                        hs = slice(h * BLOCK, (h + 1) * BLOCK)
                        rows[i, 0:1, hs] = aux[j : j + 1, rs] * LOG2E
                        rows[i, 1:2, hs] = aux[2 + j : 3 + j, rs]
        for n, k in enumerate(offsets):
            cp = pltpu.make_async_copy(kvs[n], kv.at[pl.ds(n * CHUNK, CHUNK), :], sem)
            cp.start()
            copies.append(cp)
            zk = lax.rem(z - k + NZ, NZ)
            for b in range(4):
                hb = n * 4 + b
                tags[hb] = hb + (bo[4 * (2 * zk + c) + b] << 8)
        acc[...] = jnp.zeros_like(acc)
        if first:
            dqt[...] = jnp.zeros_like(dqt)
        else:
            dqt[...] = dq_in[...]

        sub = lax.broadcasted_iota(jnp.int32, (HALF, BLOCK), 0)
        offs = (sub // 16) * 32 + 16 * p + sub % 16
        lane = lax.broadcasted_iota(jnp.int32, (1, BLOCK), 1)

        def scan(i, n):
            cq = jnp.where(i < 4, c, 1 - c)
            bq = bo[4 * (2 * z + cq) + (i & 3)]
            head = bq * BLOCK
            start0 = jnp.int32(0)
            pos_row = lane + head
            start_row = jnp.zeros_like(pos_row)
            for d in range(DOCS):
                s = sd[d]
                start0 = jnp.where(s <= head, jnp.maximum(start0, s), start0)
                start_row = jnp.where(s <= pos_row, jnp.maximum(start_row, s), start_row)
            spans[i, 0:1, :] = pos_row
            spans[i, 1:2, :] = start_row
            b0 = start0 // BLOCK
            mark = i << 20
            for hb in range(nk):
                tag = tags[hb]
                bk = tag >> 8
                cd = code[bq, bk]
                act = (bk <= bq) & (bk >= b0) & (cd != 0)
                lst[n] = tag + (cd << 16) + mark
                n = n + act.astype(jnp.int32)
            for e in range(3):
                lst[n + e] = mark
            return (n + 3) & -4

        n = lax.fori_loop(0, NQ, scan, jnp.int32(0))
        for e in range(4 * (UNROLL - 1)):
            lst[n + e] = 0
        for cp in copies:
            cp.wait()

        def tile(t, u):
            hbs, bases, bits = [], [], []
            i = lst[4 * t] >> 20
            for m in range(4):
                word = lst[4 * t + m]
                hb = pl.multiple_of((word & 255) * HALF, HALF)
                hbs.append(hb)
                bases.append(((word >> 8) & 255) * BLOCK)
                bits.append(word >> 16)
                kvt[u, m * HALF : (m + 1) * HALF, :] = kv[pl.ds(hb, HALF), :]
            keys = kvt[u, :, 0:D]
            vals = kvt[u, :, D : 2 * D]
            pos_row = spans[i, 0:1, :]
            start_row = spans[i, 1:2, :]
            nt = (((1,), (1,)), ((), ()))
            st = lax.dot_general(keys, qs[i], nt, preferred_element_type=jnp.float32)
            dpt = lax.dot_general(vals, gs[i], nt, preferred_element_type=jnp.float32)
            for h in range(4):
                hc = slice(h * BLOCK, (h + 1) * BLOCK)
                lse = rows[i, 0:1, hc]
                delta = rows[i, 1:2, hc]
                for m in range(4):
                    mr = slice(m * HALF, (m + 1) * HALF)
                    up = jnp.where((bits[m] >> h) & 1 == 1, pos_row - bases[m], -1)
                    lo = start_row - bases[m]
                    mask = (offs <= up) & (offs >= lo)
                    w = jnp.where(mask, jnp.exp2(st[mr, hc] * (SCALE * LOG2E) - lse), 0.0)
                    pt[u, mr, hc] = w.astype(jnp.bfloat16)
                    dst[u, mr, hc] = (w * (dpt[mr, hc] - delta)).astype(jnp.bfloat16)
            nn = (((1,), (0,)), ((), ()))
            dk = lax.dot_general(dst[u], qs[i], nn, preferred_element_type=jnp.float32)
            dv = lax.dot_general(pt[u], gs[i], nn, preferred_element_type=jnp.float32)
            dq = lax.dot_general(
                keys, dst[u], (((0,), (0,)), ((), ())), preferred_element_type=jnp.float32
            )
            return i, hbs, dk, dv, dq

        def tiles(t, _):
            done = [tile(UNROLL * t + u, u) for u in range(UNROLL)]
            for i, hbs, dk, dv, dq in done:
                dqt[i] += dq
                for m in range(4):
                    mr = slice(m * HALF, (m + 1) * HALF)
                    acc[pl.ds(hbs[m], HALF), 0:D] += dk[mr, :]
                    acc[pl.ds(hbs[m], HALF), D : 2 * D] += dv[mr, :]
            return 0

        lax.fori_loop(0, (n // 4 + UNROLL - 1) // UNROLL, tiles, 0)

        for n in range(nc):
            cr = slice(n * CHUNK, (n + 1) * CHUNK)
            dest = outs[n]
            dest[:, 0:D] = (acc[cr, 0:D] * SCALE).astype(dest.dtype)
            dest[:, D : 2 * D] = acc[cr, D : 2 * D].astype(dest.dtype)

    return kernel


def attend(offsets, first, bo, sd, code, meta, aux, kvs, before):
    nc = len(offsets)
    smem = pl.BlockSpec(memory_space=pltpu.SMEM)
    vmem = pl.BlockSpec(memory_space=pltpu.VMEM)
    hbm = pl.BlockSpec(memory_space=pltpu.HBM)
    shapes = [jax.ShapeDtypeStruct((NQ, D, ROWS), jnp.float32)] + [
        jax.ShapeDtypeStruct((CHUNK, 2 * D), jnp.bfloat16 if k else jnp.float32) for k in offsets
    ]
    if first:
        shapes += [jax.ShapeDtypeStruct((NQ, ROWS, D), jnp.bfloat16)] * 2
    return pl.pallas_call(
        make_kernel(offsets, first),
        in_specs=[smem] * 4 + [hbm if first else vmem] * len(before) + [vmem] * 4 + [hbm] * nc,
        out_specs=[vmem] * len(shapes),
        out_shape=shapes,
        scratch_shapes=[
            pltpu.VMEM((NQ, 8, ROWS), jnp.float32),
            pltpu.VMEM((NQ, 8, BLOCK), jnp.int32),
            pltpu.VMEM((nc * CHUNK, 2 * D), jnp.bfloat16),
            pltpu.VMEM((nc * CHUNK, 2 * D), jnp.float32),
            pltpu.VMEM((UNROLL, CHUNK, ROWS), jnp.bfloat16),
            pltpu.VMEM((UNROLL, CHUNK, ROWS), jnp.bfloat16),
            pltpu.VMEM((UNROLL, CHUNK, 2 * D), jnp.bfloat16),
            pltpu.SMEM((4 * nc,), jnp.int32),
            pltpu.SMEM((NQ * 4 * nc + 4 * UNROLL + 4,), jnp.int32),
            pltpu.SemaphoreType.DMA,
        ],
        compiler_params=pltpu.CompilerParams(vmem_limit_bytes=16 * 1024 * 1024),
        name="attend_first" if first else "attend_second",
    )(bo, sd, code, meta, *before, *aux, *kvs)


def pack_kernel(keys_in, values_in, out, keys, values, sem):
    copies = [pltpu.make_async_copy(keys_in, keys, sem), pltpu.make_async_copy(values_in, values, sem)]
    for cp in copies:
        cp.start()
    for cp in copies:
        cp.wait()
    for g in range(8):
        for half in range(2):
            r, cols = slice(16 * half, 16 * half + 16), slice(g * D, (g + 1) * D)
            out[2 * g + half, :, 0:D] = keys[r, cols]
            out[2 * g + half, :, D : 2 * D] = values[r, cols]


def flip_kernel(dq, other, mate, out):
    for b in range(4):
        for j in range(2):
            cols = slice(j * BLOCK, (j + 1) * BLOCK)
            part = dq[b, :, cols] + other[b, :, cols] + mate[b, :, cols].astype(jnp.float32)
            out[b * BLOCK : (b + 1) * BLOCK, j * D : (j + 1) * D] = part.T * SCALE


def flip(dq, other, mate):
    half = pl.BlockSpec((4, D, 2 * BLOCK), lambda i: (0, 0, 0))
    return pl.pallas_call(
        flip_kernel,
        grid=(1,),
        in_specs=[half] * 3,
        out_specs=pl.BlockSpec((4 * BLOCK, 2 * D), lambda i: (0, 0)),
        out_shape=jax.ShapeDtypeStruct((4 * BLOCK, 2 * D), jnp.float32),
        compiler_params=pltpu.CompilerParams(vmem_limit_bytes=8 * 1024 * 1024),
        name="flip",
    )(dq, other, mate)


def pack(keys, values):
    hbm = pl.BlockSpec(memory_space=pltpu.HBM)
    return pl.pallas_call(
        pack_kernel,
        in_specs=[hbm, hbm],
        out_specs=pl.BlockSpec(memory_space=pltpu.VMEM),
        scratch_shapes=[
            pltpu.VMEM(keys.shape, keys.dtype),
            pltpu.VMEM(values.shape, values.dtype),
            pltpu.SemaphoreType.DMA,
        ],
        out_shape=jax.ShapeDtypeStruct((16, 16, 2 * D), jnp.bfloat16),
        compiler_params=pltpu.CompilerParams(vmem_limit_bytes=4 * 1024 * 1024),
        name="pack",
    )(keys, values)


SWAP = [(0, 1), (1, 0)]


def turn(k):
    return [(i, (i + k) % NZ) for i in range(NZ)]


def body(
    queries, keys, values, attn_out, out_grad, log_norm, block_layout, document_ids, block_order
):
    z = lax.axis_index("z")
    c = lax.axis_index("c")
    p = lax.axis_index("p")
    meta = jnp.stack([z, c, p]).astype(jnp.int32)

    kv = pack(keys, values)
    kv = lax.all_to_all(kv, HEAD, 0, 0, tiled=True).reshape(CHUNK, 2 * D)
    kvs = {0: kv}
    for kk in INS:
        kvs[kk] = lax.ppermute(kv, "z", turn(kk))

    qg0 = jnp.concatenate([queries, out_grad], axis=1)
    qg2 = lax.ppermute(qg0, "p", SWAP)
    qg1 = lax.ppermute(qg0, "c", SWAP)
    qg3 = lax.ppermute(qg2, "c", SWAP)
    delta = jnp.sum(
        (out_grad.astype(jnp.float32) * attn_out.astype(jnp.float32)).reshape(512, 2, D), axis=2
    ).T
    aux0 = jnp.concatenate([log_norm, delta], axis=0)
    aux2 = lax.ppermute(aux0, "p", SWAP)
    aux1 = lax.ppermute(aux0, "c", SWAP)
    aux3 = lax.ppermute(aux2, "c", SWAP)
    code0 = block_layout[0] + 2 * block_layout[1]
    code2 = lax.ppermute(code0, "p", SWAP)
    code = code0 + 4 * code2
    docs = jnp.arange(DOCS, dtype=jnp.int32)
    sd = jnp.sum((document_ids[None, :] < docs[:, None]).astype(jnp.int32), axis=1)

    common = (block_order, sd, code, meta, (aux0, aux1, aux2, aux3))
    pooled = (queries, out_grad, qg1, qg2, qg3)
    dq, own, *parts, qs, gs = attend(FIRST, True, *common, [kvs[kk] for kk in FIRST], pooled)
    back = {}
    for kk, part in zip(FIRST[1:], parts):
        back[kk] = lax.ppermute(part, "z", turn(-kk))
    dq, *parts = attend(SECOND, False, *common, [kvs[kk] for kk in SECOND], (qs, gs, dq))
    other = lax.ppermute(dq[4:], "c", SWAP)
    high = (dq[:4, :, 2 * BLOCK :] + other[:, :, 2 * BLOCK :]).astype(jnp.bfloat16)
    parts[-1], high = lax.optimization_barrier((parts[-1], high))
    for kk, part in zip(SECOND, parts):
        back[kk] = lax.ppermute(part, "z", turn(-kk))
    mate = lax.ppermute(high, "p", SWAP)
    query_grad = flip(dq, other, mate)

    total = own
    for kk in INS:
        total = total + back[kk].astype(jnp.float32)
    out = lax.all_to_all(total.reshape(16, 16, 2 * D), HEAD, 0, 0, tiled=True)
    out = out.reshape(8, 2, 16, 2 * D).transpose(1, 2, 0, 3)
    key_grad = out[..., :D].reshape(32, 8 * D)
    value_grad = out[..., D:].reshape(32, 8 * D)
    return query_grad, key_grad, value_grad


def solution(mesh):
    fine = Mesh(mesh.devices.reshape(NZ, 2, 4, 2, 2), ("z", "c") + HEAD)
    seq = ("z", "c")
    in_specs = (
        P(seq, HEAD),
        P(seq + HEAD, None),
        P(seq + HEAD, None),
        P(seq, HEAD),
        P(seq, HEAD),
        P(HEAD, seq),
        P(HEAD, None, None),
        P(),
        P(),
    )
    out_specs = (P(seq, HEAD), P(seq + HEAD, None), P(seq + HEAD, None))

    return jax.shard_map(body, mesh=fine, in_specs=in_specs, out_specs=out_specs, check_vma=False)
```

profile of v0, /device:TPU:8, one launch (start us, length us, event | category | flops | bytes accessed | tf_op | source)
XLA Modules:
  0.0 116.0 jit_solution(17031880685109600061)
XLA Ops:
  0.6 1.0 constant_dynamic-update-slice_fusion.1
  1.6 0.0 copy-start.5
  1.7 1.0 constant_dynamic-update-slice_fusion
  2.7 2.2 %collective-permute-start.2 = (bf16[512,512]{1,0:T(8,128)(2,1)S(1)}, bf16[512,512]{1,0:T(8,128)(2,1)S(1)}, u32[]{:S(2)}, u32[]{:S(2)}) collective-permute-start(bf16[512,512]{1,0:T(8,128)(2,1)S(1)} %constant_dynamic-update-slice_fusion), channel_id=1, source_target_pairs={{0,1},{1,0},{2,3},{3,2},{4,5},{5,4},{6,7},{7,6},{8,9},{9,8},{10,11... | collective-permute-start | bytes 1572872 | tf_op jit(solution)/shard_map/ppermute | solution.py:288
  4.9 0.8 add_bitcast_fusion
  5.7 0.1 collective-permute-start
  5.8 0.8 copy-done.2
  6.7 0.8 copy-done.3
  7.5 0.8 pack.1
  8.3 7.2 %all-to-all-start = ((bf16[16,16,256]{2,1,0:T(8,128)(2,1)}), bf16[16,16,256]{2,1,0:T(8,128)(2,1)S(1)}, u32[]{:S(2)}, u32[]{:S(2)}) async-start(bf16[16,16,256]{2,1,0:T(8,128)(2,1)} %pack.1), calls=%async_computation | async-start | bytes 262144 | tf_op jit(solution)/shard_map/all_to_all | solution.py:282
  15.5 1.1 convert_multiply_fusion
  16.6 0.3 reshape.28
  16.9 0.6 reduce_sum.19
  17.5 0.1 copy.15
  17.6 0.1 collective-permute-start.3
  17.7 0.2 collective-permute-start.5
  17.9 0.5 collective-permute-start.4
  18.4 3.1 %collective-permute-done.5.refs_7_.refs_5_ = f32[4,512]{1,0:T(4,128)S(1)} collective-permute-done((f32[4,512]{1,0:T(4,128)S(1)}, f32[4,512]{1,0:T(4,128)S(1)}, u32[]{:S(2)}, u32[]{:S(2)}) %collective-permute-start.5) | collective-permute-done | bytes 8224 | tf_op jit(solution)/shard_map/ppermute | solution.py:295
  21.4 0.5 all-to-all-done
  21.9 6.7 %collective-permute-start.9 = (bf16[256,256]{1,0:T(8,128)(2,1)S(1)}, bf16[256,256]{1,0:T(8,128)(2,1)S(1)}, u32[]{:S(2)}, u32[]{:S(2)}) collective-permute-start(bf16[256,256]{1,0:T(8,128)(2,1)S(1)} %bitcast.22), channel_id=1, source_target_pairs={{0,160},{32,192},{64,224},{96,0},{128,32},{160,64},{192,96},{224,1... | collective-permute-start | bytes 393224 | tf_op jit(solution)/shard_map/ppermute | solution.py:285
  28.7 4.3 %collective-permute-start.7 = (bf16[256,256]{1,0:T(8,128)(2,1)S(1)}, bf16[256,256]{1,0:T(8,128)(2,1)S(1)}, u32[]{:S(2)}, u32[]{:S(2)}) collective-permute-start(bf16[256,256]{1,0:T(8,128)(2,1)S(1)} %bitcast.24), channel_id=1, source_target_pairs={{0,128},{32,160},{64,192},{96,224},{128,0},{160,32},{192,64},{224,... | collective-permute-start | bytes 393224 | tf_op jit(solution)/shard_map/ppermute | solution.py:285
  32.9 0.1 pad_add_fusion.meta
  33.0 0.2 convert_reduce_fusion.sd
  33.2 9.7 %collective-permute-done.9.refs_12_ = bf16[256,256]{1,0:T(8,128)(2,1)S(1)} collective-permute-done((bf16[256,256]{1,0:T(8,128)(2,1)S(1)}, bf16[256,256]{1,0:T(8,128)(2,1)S(1)}, u32[]{:S(2)}, u32[]{:S(2)}) %collective-permute-start.9) | collective-permute-done | bytes 131104 | tf_op jit(solution)/shard_map/ppermute | solution.py:285
  42.9 3.3 %collective-permute-done.8.refs_11_ = bf16[256,256]{1,0:T(8,128)(2,1)S(1)} collective-permute-done((bf16[256,256]{1,0:T(8,128)(2,1)S(1)}, bf16[256,256]{1,0:T(8,128)(2,1)S(1)}, u32[]{:S(2)}, u32[]{:S(2)}) %collective-permute-start.8) | collective-permute-done | bytes 131104 | tf_op jit(solution)/shard_map/ppermute | solution.py:285
  46.1 2.9 %collective-permute-start.11 = (bf16[256,256]{1,0:T(8,128)(2,1)S(1)}, bf16[256,256]{1,0:T(8,128)(2,1)S(1)}, u32[]{:S(2)}, u32[]{:S(2)}) collective-permute-start(bf16[256,256]{1,0:T(8,128)(2,1)S(1)} %bitcast.27), channel_id=1, source_target_pairs={{0,192},{32,224},{64,0},{96,32},{128,64},{160,96},{192,128},{224,1... | collective-permute-start | bytes 393224 | tf_op jit(solution)/shard_map/ppermute | solution.py:285
  49.0 0.7 collective-permute-start.10
  49.8 10.2 %attend_first.1 = (f32[8,128,512]{2,1,0:T(8,128)S(1)}, f32[256,256]{1,0:T(8,128)S(1)}, bf16[256,256]{1,0:T(8,128)(2,1)S(1)}, bf16[256,256]{1,0:T(8,128)(2,1)S(1)...) custom-call(s32[64]{0:T(128)S(1)} %copy-done.4, ...), custom_call_target="tpu_custom_call" | custom-call | tf_op jit(solution)/shard_map/attend_first/pallas_call | solution.py:193
  60.1 8.1 %attend_second.1 = (f32[8,128,512]{2,1,0:T(8,128)S(1)}, bf16[256,256]{1,0:T(8,128)(2,1)S(1)}, bf16[256,256]{1,0:T(8,128)(2,1)S(1)}, bf16[256,256]{1,0:T(8,128)(2,1)S(1)}, bf16[256,256]{1,0:T(8,128)(2,1)S(1)}) custom-call(s32[64]{0:T(128)S(1)} %copy-done.4, s32[8]{0:T(128)S(1)} %convert_reduce_fusion.sd, s32[64,64]{1,0:T(8,128)S(1)} %multiply_add_fusion.code, ...), custom_call_target="tpu_custom_call" | custom-call | tf_op jit(solution)/shard_map/attend_second/pallas_call | solution.py:193
  68.1 0.1 slice.23
  68.2 0.1 collective-permute-start.14
  68.3 2.1 %collective-permute-start.19 = (bf16[256,256]{1,0:T(8,128)(2,1)S(1)}, bf16[256,256]{1,0:T(8,128)(2,1)S(1)}, u32[]{:S(2)}, u32[]{:S(2)}) collective-permute-start(bf16[256,256]{1,0:T(8,128)(2,1)S(1)} %get-tuple-element.27), channel_id=1, source_target_pairs={{0,192},{32,224},{64,0},{96,32},{128,64},{160,96},{192,128},{224,1... | collective-permute-start | bytes 393224 | tf_op jit(solution)/shard_map/ppermute | solution.py:315
  70.4 0.9 collective-permute-start.20
  71.3 6.5 %collective-permute-start.21 = (bf16[256,256]{1,0:T(8,128)(2,1)S(1)}, bf16[256,256]{1,0:T(8,128)(2,1)S(1)}, u32[]{:S(2)}, u32[]{:S(2)}) collective-permute-start(bf16[256,256]{1,0:T(8,128)(2,1)S(1)} %get-tuple-element.29), channel_id=1, source_target_pairs={{0,224},{32,0},{64,32},{96,64},{128,96},{160,128},{192,160},{224,1... | collective-permute-start | bytes 393224 | tf_op jit(solution)/shard_map/ppermute | solution.py:315
  77.8 1.8 %collective-permute-start.17 = (bf16[256,256]{1,0:T(8,128)(2,1)S(1)}, bf16[256,256]{1,0:T(8,128)(2,1)S(1)}, u32[]{:S(2)}, u32[]{:S(2)}) collective-permute-start(bf16[256,256]{1,0:T(8,128)(2,1)S(1)} %get-tuple-element.25), channel_id=1, source_target_pairs={{0,160},{32,192},{64,224},{96,0},{128,32},{160,64},{192,96},{224,1... | collective-permute-start | bytes 393224 | tf_op jit(solution)/shard_map/ppermute | solution.py:309
  79.6 0.8 fusion
  80.4 2.0 %collective-permute-start.18 = (bf16[256,256]{1,0:T(8,128)(2,1)S(1)}, bf16[256,256]{1,0:T(8,128)(2,1)S(1)}, u32[]{:S(2)}, u32[]{:S(2)}) collective-permute-start(bf16[256,256]{1,0:T(8,128)(2,1)S(1)} %get-tuple-element.26), channel_id=1, source_target_pairs={{0,96},{32,128},{64,160},{96,192},{128,224},{160,0},{192,32},{224,... | collective-permute-start | bytes 393224 | tf_op jit(solution)/shard_map/ppermute | solution.py:309
  82.5 10.0 %collective-permute-start.22 = (bf16[256,256]{1,0:T(8,128)(2,1)S(1)}, bf16[256,256]{1,0:T(8,128)(2,1)S(1)}, u32[]{:S(2)}, u32[]{:S(2)}) collective-permute-start(bf16[256,256]{1,0:T(8,128)(2,1)S(1)} %get-tuple-element.30), channel_id=1, source_target_pairs={{0,32},{32,64},{64,96},{96,128},{128,160},{160,192},{192,224},{224... | collective-permute-start | bytes 393224 | tf_op jit(solution)/shard_map/ppermute | solution.py:315
  92.5 0.7 collective-permute-start.15
  93.1 2.5 %collective-permute-done.17 = bf16[256,256]{1,0:T(8,128)(2,1)S(1)} collective-permute-done((bf16[256,256]{1,0:T(8,128)(2,1)S(1)}, bf16[256,256]{1,0:T(8,128)(2,1)S(1)}, u32[]{:S(2)}, u32[]{:S(2)}) %collective-permute-start.17) | collective-permute-done | bytes 131104 | tf_op jit(solution)/shard_map/ppermute | solution.py:309
  95.7 1.3 %collective-permute-done.18 = bf16[256,256]{1,0:T(8,128)(2,1)S(1)} collective-permute-done((bf16[256,256]{1,0:T(8,128)(2,1)S(1)}, bf16[256,256]{1,0:T(8,128)(2,1)S(1)}, u32[]{:S(2)}, u32[]{:S(2)}) %collective-permute-start.18) | collective-permute-done | bytes 131104 | tf_op jit(solution)/shard_map/ppermute | solution.py:309
  97.0 2.0 %collective-permute-done.22 = bf16[256,256]{1,0:T(8,128)(2,1)S(1)} collective-permute-done((bf16[256,256]{1,0:T(8,128)(2,1)S(1)}, bf16[256,256]{1,0:T(8,128)(2,1)S(1)}, u32[]{:S(2)}, u32[]{:S(2)}) %collective-permute-start.22) | collective-permute-done | bytes 131104 | tf_op jit(solution)/shard_map/ppermute | solution.py:315
  99.0 0.8 convert_add_fusion
  99.8 7.2 %all-to-all-start.1 = ((f32[16,16,256]{2,1,0:T(8,128)}), f32[16,16,256]{2,1,0:T(8,128)}, u32[]{:S(2)}, u32[]{:S(2)}) async-start(f32[16,16,256]{2,1,0:T(8,128)} %bitcast.31), calls=%async_computation.1 | async-start | bytes 524288 | tf_op jit(solution)/shard_map/all_to_all | solution.py:322
  107.0 1.0 flip.1
  108.0 6.1 %all-to-all-done.1 = f32[16,16,256]{2,1,0:T(8,128)} async-done(((f32[16,16,256]{2,1,0:T(8,128)}), f32[16,16,256]{2,1,0:T(8,128)}, u32[]{:S(2)}, u32[]{:S(2)}) %all-to-all-start.1) | async-done | bytes 262176 | tf_op jit(solution)/shard_map/all_to_all | solution.py:322
  114.1 1.1 copy.22
  115.2 0.7 copy_bitcast_fusion.1
  (39 shorter events, 0.1 us)
Async XLA Ops:
  1.6 16.1 %copy-start.7 = (f32[2,512]{1,0:T(2,128)S(1)}, f32[2,512]{1,0:T(2,128)}, u32[]{:S(2)}) copy-start(f32[2,512]{1,0:T(2,128)} %param.14) | copy-start | bytes 12292
  1.6 31.4 %copy-start.6 = (s32[8192]{0:T(1024)S(1)}, s32[8192]{0:T(1024)}, u32[]{:S(2)}) copy-start(s32[8192]{0:T(1024)} %param.16) | copy-start | bytes 98308
  1.6 48.2 %copy-start.5 = (s32[2,64,64]{2,1,0:T(8,128)S(1)}, s32[2,64,64]{2,1,0:T(8,128)}, u32[]{:S(2)}) copy-start(s32[2,64,64]{2,1,0:T(8,128)} %param.15) | copy-start | bytes 98308
  1.6 48.2 %copy-start.4 = (s32[64]{0:T(128)S(1)}, s32[64]{0:T(128)}, u32[]{:S(2)}) copy-start(s32[64]{0:T(128)} %bo.3) | copy-start | bytes 772
  2.7 47.2 %copy-start = (bf16[512,256]{1,0:T(8,128)(2,1)S(1)}, bf16[512,256]{1,0:T(8,128)(2,1)}, u32[]{:S(2)}) copy-start(bf16[512,256]{1,0:T(8,128)(2,1)} %refs_1_.1) | copy-start | bytes 786436
  2.7 47.2 %copy-start.1 = (bf16[512,256]{1,0:T(8,128)(2,1)S(1)}, bf16[512,256]{1,0:T(8,128)(2,1)}, u32[]{:S(2)}) copy-start(bf16[512,256]{1,0:T(8,128)(2,1)} %refs_0_.1) | copy-start | bytes 786436
  2.7 14.9 %collective-permute-start.2 = (bf16[512,512]{1,0:T(8,128)(2,1)S(1)}, bf16[512,512]{1,0:T(8,128)(2,1)S(1)}, u32[]{:S(2)}, u32[]{:S(2)}) collective-permute-start(bf16[512,512]{1,0:T(8,128)(2,1)S(1)} %constant_dynamic-update-slice_fusion), channel_id=1, source_target_pairs={{0,1},{1,0},{2,3},{3,2},{4,5},{5,4},{6,7},{7,6},{8,9},{9,8},{10,11... | collective-permute-start | bytes 1572872 | tf_op jit(solution)/shard_map/ppermute | solution.py:288
  4.9 44.1 %collective-permute-start.1 = (bf16[512,512]{1,0:T(8,128)(2,1)S(1)}, bf16[512,512]{1,0:T(8,128)(2,1)S(1)}, u32[]{:S(2)}, u32[]{:S(2)}) collective-permute-start(bf16[512,512]{1,0:T(8,128)(2,1)S(1)} %constant_dynamic-update-slice_fusion), channel_id=1, source_target_pairs={{0,16},{16,0},{1,17},{17,1},{2,18},{18,2},{3,19},{19,3},{4,20},{20... | collective-permute-start | bytes 1572872 | tf_op jit(solution)/shard_map/ppermute | solution.py:289
  5.7 22.9 %collective-permute-start = (s32[64,64]{1,0:T(8,128)S(1)}, s32[64,64]{1,0:T(8,128)S(1)}, u32[]{:S(2)}, u32[]{:S(2)}) collective-permute-start(s32[64,64]{1,0:T(8,128)S(1)} %add_bitcast_fusion), channel_id=1, source_target_pairs={{0,1},{1,0},{2,3},{3,2},{4,5},{5,4},{6,7},{7,6},{8,9},{9,8},{10,11... | collective-permute-start | bytes 49160 | tf_op jit(solution)/shard_map/ppermute | solution.py:299
  5.8 0.8 copy-start.2
  6.7 0.8 copy-start.3
  8.3 13.6 %all-to-all-start = ((bf16[16,16,256]{2,1,0:T(8,128)(2,1)}), bf16[16,16,256]{2,1,0:T(8,128)(2,1)S(1)}, u32[]{:S(2)}, u32[]{:S(2)}) async-start(bf16[16,16,256]{2,1,0:T(8,128)(2,1)} %pack.1), calls=%async_computation | async-start | bytes 262144 | tf_op jit(solution)/shard_map/all_to_all | solution.py:282
  17.6 32.2 %collective-permute-start.3 = (bf16[512,512]{1,0:T(8,128)(2,1)S(1)}, bf16[512,512]{1,0:T(8,128)(2,1)S(1)}, u32[]{:S(2)}, u32[]{:S(2)}) collective-permute-start(bf16[512,512]{1,0:T(8,128)(2,1)S(1)} %collective-permute-done.2.refs_3_), channel_id=1, source_target_pairs={{0,16},{16,0},{1,17},{17,1},{2,18},{18,2},{3,19},{19,3},{4,20},{20... | collective-permute-start | bytes 1572872 | tf_op jit(solution)/shard_map/ppermute | solution.py:290
  17.7 3.7 %collective-permute-start.5 = (f32[4,512]{1,0:T(4,128)S(1)}, f32[4,512]{1,0:T(4,128)S(1)}, u32[]{:S(2)}, u32[]{:S(2)}) collective-permute-start(f32[4,512]{1,0:T(4,128)S(1)} %pad_maximum_fusion.refs_5_.refs_3_), channel_id=1, source_target_pairs={{0,1},{1,0},{2,3},{3,2},{4,5},{5,4},{6,7},{7,6},{8,9},{9,8},{10,11... | collective-permute-start | bytes 24584 | tf_op jit(solution)/shard_map/ppermute | solution.py:295
  17.9 3.6 %collective-permute-start.4 = (f32[4,512]{1,0:T(4,128)S(1)}, f32[4,512]{1,0:T(4,128)S(1)}, u32[]{:S(2)}, u32[]{:S(2)}) collective-permute-start(f32[4,512]{1,0:T(4,128)S(1)} %pad_maximum_fusion.refs_5_.refs_3_), channel_id=1, source_target_pairs={{0,16},{16,0},{1,17},{17,1},{2,18},{18,2},{3,19},{19,3},{4,20},{20... | collective-permute-start | bytes 24584 | tf_op jit(solution)/shard_map/ppermute | solution.py:296
  21.4 7.2 %collective-permute-start.6 = (f32[4,512]{1,0:T(4,128)S(1)}, f32[4,512]{1,0:T(4,128)S(1)}, u32[]{:S(2)}, u32[]{:S(2)}) collective-permute-start(f32[4,512]{1,0:T(4,128)S(1)} %collective-permute-done.5.refs_7_.refs_5_), channel_id=1, source_target_pairs={{0,16},{16,0},{1,17},{17,1},{2,18},{18,2},{3,19},{19,3},{4,20},{20... | collective-permute-start | bytes 24584 | tf_op jit(solution)/shard_map/ppermute | solution.py:297
  21.9 21.0 %collective-permute-start.9 = (bf16[256,256]{1,0:T(8,128)(2,1)S(1)}, bf16[256,256]{1,0:T(8,128)(2,1)S(1)}, u32[]{:S(2)}, u32[]{:S(2)}) collective-permute-start(bf16[256,256]{1,0:T(8,128)(2,1)S(1)} %bitcast.22), channel_id=1, source_target_pairs={{0,160},{32,192},{64,224},{96,0},{128,32},{160,64},{192,96},{224,1... | collective-permute-start | bytes 393224 | tf_op jit(solution)/shard_map/ppermute | solution.py:285
  28.6 17.5 %collective-permute-start.8 = (bf16[256,256]{1,0:T(8,128)(2,1)S(1)}, bf16[256,256]{1,0:T(8,128)(2,1)S(1)}, u32[]{:S(2)}, u32[]{:S(2)}) collective-permute-start(bf16[256,256]{1,0:T(8,128)(2,1)S(1)} %bitcast.23), channel_id=1, source_target_pairs={{0,96},{32,128},{64,160},{96,192},{128,224},{160,0},{192,32},{224,... | collective-permute-start | bytes 393224 | tf_op jit(solution)/shard_map/ppermute | solution.py:285
  28.7 17.5 %collective-permute-start.7 = (bf16[256,256]{1,0:T(8,128)(2,1)S(1)}, bf16[256,256]{1,0:T(8,128)(2,1)S(1)}, u32[]{:S(2)}, u32[]{:S(2)}) collective-permute-start(bf16[256,256]{1,0:T(8,128)(2,1)S(1)} %bitcast.24), channel_id=1, source_target_pairs={{0,128},{32,160},{64,192},{96,224},{128,0},{160,32},{192,64},{224,... | collective-permute-start | bytes 393224 | tf_op jit(solution)/shard_map/ppermute | solution.py:285
  42.9 17.2 %collective-permute-start.13 = (bf16[256,256]{1,0:T(8,128)(2,1)S(1)}, bf16[256,256]{1,0:T(8,128)(2,1)S(1)}, u32[]{:S(2)}, u32[]{:S(2)}) collective-permute-start(bf16[256,256]{1,0:T(8,128)(2,1)S(1)} %bitcast.25), channel_id=1, source_target_pairs={{0,224},{32,0},{64,32},{96,64},{128,96},{160,128},{192,160},{224,1... | collective-permute-start | bytes 393224 | tf_op jit(solution)/shard_map/ppermute | solution.py:285
  46.1 13.9 %collective-permute-start.12 = (bf16[256,256]{1,0:T(8,128)(2,1)S(1)}, bf16[256,256]{1,0:T(8,128)(2,1)S(1)}, u32[]{:S(2)}, u32[]{:S(2)}) collective-permute-start(bf16[256,256]{1,0:T(8,128)(2,1)S(1)} %bitcast.26), channel_id=1, source_target_pairs={{0,32},{32,64},{64,96},{96,128},{128,160},{160,192},{192,224},{224... | collective-permute-start | bytes 393224 | tf_op jit(solution)/shard_map/ppermute | solution.py:285
  46.1 13.9 %collective-permute-start.11 = (bf16[256,256]{1,0:T(8,128)(2,1)S(1)}, bf16[256,256]{1,0:T(8,128)(2,1)S(1)}, u32[]{:S(2)}, u32[]{:S(2)}) collective-permute-start(bf16[256,256]{1,0:T(8,128)(2,1)S(1)} %bitcast.27), channel_id=1, source_target_pairs={{0,192},{32,224},{64,0},{96,32},{128,64},{160,96},{192,128},{224,1... | collective-permute-start | bytes 393224 | tf_op jit(solution)/shard_map/ppermute | solution.py:285
  49.0 11.0 %collective-permute-start.10 = (bf16[256,256]{1,0:T(8,128)(2,1)S(1)}, bf16[256,256]{1,0:T(8,128)(2,1)S(1)}, u32[]{:S(2)}, u32[]{:S(2)}) collective-permute-start(bf16[256,256]{1,0:T(8,128)(2,1)S(1)} %bitcast.28), channel_id=1, source_target_pairs={{0,64},{32,96},{64,128},{96,160},{128,192},{160,224},{192,0},{224,... | collective-permute-start | bytes 393224 | tf_op jit(solution)/shard_map/ppermute | solution.py:285
  68.2 9.6 %collective-permute-start.14 = (f32[4,128,512]{2,1,0:T(8,128)S(1)}, f32[4,128,512]{2,1,0:T(8,128)S(1)}, u32[]{:S(2)}, u32[]{:S(2)}) collective-permute-start(f32[4,128,512]{2,1,0:T(8,128)S(1)} %slice.23), channel_id=1, source_target_pairs={{0,16},{16,0},{1,17},{17,1},{2,18},{18,2},{3,19},{19,3},{4,20},{20... | collective-permute-start | bytes 3145736 | tf_op jit(solution)/shard_map/ppermute | solution.py:311
  68.3 12.1 %collective-permute-start.19 = (bf16[256,256]{1,0:T(8,128)(2,1)S(1)}, bf16[256,256]{1,0:T(8,128)(2,1)S(1)}, u32[]{:S(2)}, u32[]{:S(2)}) collective-permute-start(bf16[256,256]{1,0:T(8,128)(2,1)S(1)} %get-tuple-element.27), channel_id=1, source_target_pairs={{0,192},{32,224},{64,0},{96,32},{128,64},{160,96},{192,128},{224,1... | collective-permute-start | bytes 393224 | tf_op jit(solution)/shard_map/ppermute | solution.py:315
  70.4 12.1 %collective-permute-start.20 = (bf16[256,256]{1,0:T(8,128)(2,1)S(1)}, bf16[256,256]{1,0:T(8,128)(2,1)S(1)}, u32[]{:S(2)}, u32[]{:S(2)}) collective-permute-start(bf16[256,256]{1,0:T(8,128)(2,1)S(1)} %get-tuple-element.28), channel_id=1, source_target_pairs={{0,64},{32,96},{64,128},{96,160},{128,192},{160,224},{192,0},{224,... | collective-permute-start | bytes 393224 | tf_op jit(solution)/shard_map/ppermute | solution.py:315
  71.3 21.2 %collective-permute-start.21 = (bf16[256,256]{1,0:T(8,128)(2,1)S(1)}, bf16[256,256]{1,0:T(8,128)(2,1)S(1)}, u32[]{:S(2)}, u32[]{:S(2)}) collective-permute-start(bf16[256,256]{1,0:T(8,128)(2,1)S(1)} %get-tuple-element.29), channel_id=1, source_target_pairs={{0,224},{32,0},{64,32},{96,64},{128,96},{160,128},{192,160},{224,1... | collective-permute-start | bytes 393224 | tf_op jit(solution)/shard_map/ppermute | solution.py:315
  77.8 15.3 %collective-permute-start.16 = (bf16[256,256]{1,0:T(8,128)(2,1)S(1)}, bf16[256,256]{1,0:T(8,128)(2,1)S(1)}, u32[]{:S(2)}, u32[]{:S(2)}) collective-permute-start(bf16[256,256]{1,0:T(8,128)(2,1)S(1)} %get-tuple-element.24), channel_id=1, source_target_pairs={{0,128},{32,160},{64,192},{96,224},{128,0},{160,32},{192,64},{224,... | collective-permute-start | bytes 393224 | tf_op jit(solution)/shard_map/ppermute | solution.py:309
  77.8 17.9 %collective-permute-start.17 = (bf16[256,256]{1,0:T(8,128)(2,1)S(1)}, bf16[256,256]{1,0:T(8,128)(2,1)S(1)}, u32[]{:S(2)}, u32[]{:S(2)}) collective-permute-start(bf16[256,256]{1,0:T(8,128)(2,1)S(1)} %get-tuple-element.25), channel_id=1, source_target_pairs={{0,160},{32,192},{64,224},{96,0},{128,32},{160,64},{192,96},{224,1... | collective-permute-start | bytes 393224 | tf_op jit(solution)/shard_map/ppermute | solution.py:309
  80.4 16.5 %collective-permute-start.18 = (bf16[256,256]{1,0:T(8,128)(2,1)S(1)}, bf16[256,256]{1,0:T(8,128)(2,1)S(1)}, u32[]{:S(2)}, u32[]{:S(2)}) collective-permute-start(bf16[256,256]{1,0:T(8,128)(2,1)S(1)} %get-tuple-element.26), channel_id=1, source_target_pairs={{0,96},{32,128},{64,160},{96,192},{128,224},{160,0},{192,32},{224,... | collective-permute-start | bytes 393224 | tf_op jit(solution)/shard_map/ppermute | solution.py:309
  82.5 16.5 %collective-permute-start.22 = (bf16[256,256]{1,0:T(8,128)(2,1)S(1)}, bf16[256,256]{1,0:T(8,128)(2,1)S(1)}, u32[]{:S(2)}, u32[]{:S(2)}) collective-permute-start(bf16[256,256]{1,0:T(8,128)(2,1)S(1)} %get-tuple-element.30), channel_id=1, source_target_pairs={{0,32},{32,64},{64,96},{96,128},{128,160},{160,192},{192,224},{224... | collective-permute-start | bytes 393224 | tf_op jit(solution)/shard_map/ppermute | solution.py:315
  92.5 14.5 %collective-permute-start.15 = (bf16[4,128,256]{2,1,0:T(8,128)(2,1)}, bf16[4,128,256]{2,1,0:T(8,128)(2,1)S(1)}, u32[]{:S(2)}, u32[]{:S(2)}) collective-permute-start(bf16[4,128,256]{2,1,0:T(8,128)(2,1)} %fusion), channel_id=1, source_target_pairs={{0,1},{1,0},{2,3},{3,2},{4,5},{5,4},{6,7},{7,6},{8,9},{9,8},{10,11... | collective-permute-start | bytes 786440 | tf_op jit(solution)/shard_map/ppermute | solution.py:316
  99.8 14.3 %all-to-all-start.1 = ((f32[16,16,256]{2,1,0:T(8,128)}), f32[16,16,256]{2,1,0:T(8,128)}, u32[]{:S(2)}, u32[]{:S(2)}) async-start(f32[16,16,256]{2,1,0:T(8,128)} %bitcast.31), calls=%async_computation.1 | async-start | bytes 524288 | tf_op jit(solution)/shard_map/all_to_all | solution.py:322
where the time goes:
time: 117 us; the launch traced here: 116 us
  starting transfers between devices  56.2 us (48%)
  waiting for transfers between devices  28.4 us (24%)
  Pallas kernels  20.1 us (17%)
  local copies, waits for them, and re-layouts  6.01 us (5%)
  other arithmetic  4.37 us (4%)
    ppermute x7, starting transfers between devices, body(): back[kk] = lax.ppermute(part, 'z', turn(-kk))  23.4 us
    pallas_call x2, Pallas kernels, attend(): pl.pallas_call(make_kernel(offsets, first), in_specs=[smem] * 4 + [hbm if...  18.3 us
    ppermute x7, starting transfers between devices, body(): kvs[kk] = lax.ppermute(kv, 'z', turn(kk))  14.7 us
    ppermute x7, waiting for transfers between devices, body(): kvs[kk] = lax.ppermute(kv, 'z', turn(kk))  13 us
    all_to_all x1, starting transfers between devices, body(): out = lax.all_to_all(total.reshape(16, 16, 2 * D), HEAD, 0, 0, tiled=True)  7.2 us
    all_to_all x1, starting transfers between devices, body(): kv = lax.all_to_all(kv, HEAD, 0, 0, tiled=True).reshape(CHUNK, 2 * D)  7.16 us
    all_to_all x1, waiting for transfers between devices, body(): out = lax.all_to_all(total.reshape(16, 16, 2 * D), HEAD, 0, 0, tiled=True)  6.08 us
    ppermute x7, waiting for transfers between devices, body(): back[kk] = lax.ppermute(part, 'z', turn(-kk))  5.85 us
  transfers between devices with their start and end apart: 25, of which 8 were waited for; matrix products, arithmetic and copies ran while one was open for 4% of the time, Pallas kernels for 10%

commit v1 on v0

--- a/solution.py
+++ b/solution.py
@@ -73,9 +73,7 @@
                         rows[i, 0:1, hs] = aux[j : j + 1, rs] * LOG2E
                         rows[i, 1:2, hs] = aux[2 + j : 3 + j, rs]
         for n, k in enumerate(offsets):
-            cp = pltpu.make_async_copy(kvs[n], kv.at[pl.ds(n * CHUNK, CHUNK), :], sem)
-            cp.start()
-            copies.append(cp)
+            kv[n * CHUNK : (n + 1) * CHUNK, :] = kvs[n][...]
             zk = lax.rem(z - k + NZ, NZ)
             for b in range(4):
                 hb = n * 4 + b
@@ -192,7 +190,7 @@
         shapes += [jax.ShapeDtypeStruct((NQ, ROWS, D), jnp.bfloat16)] * 2
     return pl.pallas_call(
         make_kernel(offsets, first),
-        in_specs=[smem] * 4 + [hbm if first else vmem] * len(before) + [vmem] * 4 + [hbm] * nc,
+        in_specs=[smem] * 4 + [hbm if first else vmem] * len(before) + [vmem] * (4 + nc),
         out_specs=[vmem] * len(shapes),
         out_shape=shapes,
         scratch_shapes=[
@@ -246,6 +244,26 @@
     )(dq, other, mate)
 
 
+def unpack_kernel(parts, keys, values):
+    for g in range(8):
+        for half in range(2):
+            r, cols = slice(16 * half, 16 * half + 16), slice(g * D, (g + 1) * D)
+            keys[r, cols] = parts[2 * g + half, :, 0:D]
+            values[r, cols] = parts[2 * g + half, :, D : 2 * D]
+
+
+def unpack(parts):
+    vmem = pl.BlockSpec(memory_space=pltpu.VMEM)
+    return pl.pallas_call(
+        unpack_kernel,
+        in_specs=[vmem],
+        out_specs=[vmem, vmem],
+        out_shape=[jax.ShapeDtypeStruct((32, 8 * D), jnp.float32)] * 2,
+        compiler_params=pltpu.CompilerParams(vmem_limit_bytes=4 * 1024 * 1024),
+        name="unpack",
+    )(parts)
+
+
 def pack(keys, values):
     hbm = pl.BlockSpec(memory_space=pltpu.HBM)
     return pl.pallas_call(
@@ -320,9 +338,7 @@
     for kk in INS:
         total = total + back[kk].astype(jnp.float32)
     out = lax.all_to_all(total.reshape(16, 16, 2 * D), HEAD, 0, 0, tiled=True)
-    out = out.reshape(8, 2, 16, 2 * D).transpose(1, 2, 0, 3)
-    key_grad = out[..., :D].reshape(32, 8 * D)
-    value_grad = out[..., D:].reshape(32, 8 * D)
+    key_grad, value_grad = unpack(out)
     return query_grad, key_grad, value_grad
 
 

time: 117 us -> 114 us (0.974)
  local copies, waits for them, and re-layouts: 6.01 us -> 4.14 us
    reshape x2 -> x0, local copies, waits for them, and re-layouts: 1.85 us -> none  [the longest x1 1.11 us: body(): out = out.reshape(8, 2, 16, 2 * D).transpose(1, 2, 0, 3)]
    pallas_call x2, Pallas kernels: 18.3 us -> 16.9 us  [attend(): pl.pallas_call(make_kernel(offsets, first), in_specs=[smem] * 4 + [hbm if...]
  transfers between devices with their start and end apart: 25 -> 25, of which waited for: 8 -> 8; matrix products, arithmetic and copies ran while one was open for 4% -> 4% of each run, Pallas kernels for 10% -> 11%
where the time goes in v1:
time: 114 us; the launch traced here: 113 us
  starting transfers between devices  56.2 us (49%)
  waiting for transfers between devices  27.3 us (24%)
  Pallas kernels  20.5 us (18%)
  other arithmetic  4.37 us (4%)
  local copies, waits for them, and re-layouts  4.14 us (4%)
    ppermute x7, starting transfers between devices, body(): back[kk] = lax.ppermute(part, 'z', turn(-kk))  23.3 us
    pallas_call x2, Pallas kernels, attend(): pl.pallas_call(make_kernel(offsets, first), in_specs=[smem] * 4 + [hbm if...  16.9 us
    ppermute x7, starting transfers between devices, body(): kvs[kk] = lax.ppermute(kv, 'z', turn(kk))  14.7 us
    ppermute x7, waiting for transfers between devices, body(): kvs[kk] = lax.ppermute(kv, 'z', turn(kk))  13 us
    all_to_all x1, starting transfers between devices, body(): out = lax.all_to_all(total.reshape(16, 16, 2 * D), HEAD, 0, 0, tiled=True)  7.21 us
    all_to_all x1, starting transfers between devices, body(): kv = lax.all_to_all(kv, HEAD, 0, 0, tiled=True).reshape(CHUNK, 2 * D)  7.16 us
    ppermute x7, waiting for transfers between devices, body(): back[kk] = lax.ppermute(part, 'z', turn(-kk))  5.86 us
    all_to_all x1, waiting for transfers between devices, body(): out = lax.all_to_all(total.reshape(16, 16, 2 * D), HEAD, 0, 0, tiled=True)  4.96 us
  transfers between devices with their start and end apart: 25, of which 8 were waited for; matrix products, arithmetic and copies ran while one was open for 4% of the time, Pallas kernels for 11%

profile of v1, /device:TPU:8, one launch (start us, length us, event | category | flops | bytes accessed | tf_op | source)
XLA Modules:
  0.0 113.4 jit_solution(541664281135095546)
XLA Ops:
  0.6 1.0 constant_dynamic-update-slice_fusion.1
  1.6 0.0 copy-start.5
  1.6 0.0 copy-start.4
  1.7 1.0 constant_dynamic-update-slice_fusion
  2.7 2.2 %collective-permute-start.2 = (bf16[512,512]{1,0:T(8,128)(2,1)S(1)}, bf16[512,512]{1,0:T(8,128)(2,1)S(1)}, u32[]{:S(2)}, u32[]{:S(2)}) collective-permute-start(bf16[512,512]{1,0:T(8,128)(2,1)S(1)} %constant_dynamic-update-slice_fusion), channel_id=1, source_target_pairs={{0,1},{1,0},{2,3},{3,2},{4,5},{5,4},{6,7},{7,6},{8,9},{9,8},{10,11... | collective-permute-start | bytes 1572872 | tf_op jit(solution)/shard_map/ppermute | solution.py:306
  4.9 0.8 add_bitcast_fusion
  5.7 0.1 collective-permute-start
  5.8 0.8 copy-done.2
  6.7 0.8 copy-done.3
  7.5 0.8 pack.1
  8.3 7.2 %all-to-all-start = ((bf16[16,16,256]{2,1,0:T(8,128)(2,1)}), bf16[16,16,256]{2,1,0:T(8,128)(2,1)S(1)}, u32[]{:S(2)}, u32[]{:S(2)}) async-start(bf16[16,16,256]{2,1,0:T(8,128)(2,1)} %pack.1), calls=%async_computation | async-start | bytes 262144 | tf_op jit(solution)/shard_map/all_to_all | solution.py:300
  15.5 1.1 convert_multiply_fusion
  16.6 0.3 reshape.19
  16.9 0.6 reduce_sum.19
  17.5 0.1 copy.13
  17.6 0.1 collective-permute-start.3
  17.7 0.2 collective-permute-start.5
  17.9 0.5 collective-permute-start.4
  18.4 3.1 %collective-permute-done.5.refs_7_.refs_5_ = f32[4,512]{1,0:T(4,128)S(1)} collective-permute-done((f32[4,512]{1,0:T(4,128)S(1)}, f32[4,512]{1,0:T(4,128)S(1)}, u32[]{:S(2)}, u32[]{:S(2)}) %collective-permute-start.5) | collective-permute-done | bytes 8224 | tf_op jit(solution)/shard_map/ppermute | solution.py:313
  21.4 0.5 all-to-all-done
  21.9 6.7 %collective-permute-start.9 = (bf16[256,256]{1,0:T(8,128)(2,1)S(1)}, bf16[256,256]{1,0:T(8,128)(2,1)S(1)}, u32[]{:S(2)}, u32[]{:S(2)}) collective-permute-start(bf16[256,256]{1,0:T(8,128)(2,1)S(1)} %bitcast.10), channel_id=1, source_target_pairs={{0,160},{32,192},{64,224},{96,0},{128,32},{160,64},{192,96},{224,1... | collective-permute-start | bytes 393224 | tf_op jit(solution)/shard_map/ppermute | solution.py:303
  28.7 4.3 %collective-permute-start.7 = (bf16[256,256]{1,0:T(8,128)(2,1)S(1)}, bf16[256,256]{1,0:T(8,128)(2,1)S(1)}, u32[]{:S(2)}, u32[]{:S(2)}) collective-permute-start(bf16[256,256]{1,0:T(8,128)(2,1)S(1)} %bitcast.12), channel_id=1, source_target_pairs={{0,128},{32,160},{64,192},{96,224},{128,0},{160,32},{192,64},{224,... | collective-permute-start | bytes 393224 | tf_op jit(solution)/shard_map/ppermute | solution.py:303
  32.9 0.1 pad_add_fusion.meta
  33.0 0.2 convert_reduce_fusion.sd
  33.2 9.7 %collective-permute-done.9.refs_12_ = bf16[256,256]{1,0:T(8,128)(2,1)S(1)} collective-permute-done((bf16[256,256]{1,0:T(8,128)(2,1)S(1)}, bf16[256,256]{1,0:T(8,128)(2,1)S(1)}, u32[]{:S(2)}, u32[]{:S(2)}) %collective-permute-start.9) | collective-permute-done | bytes 131104 | tf_op jit(solution)/shard_map/ppermute | solution.py:303
  42.9 3.3 %collective-permute-done.8.refs_11_ = bf16[256,256]{1,0:T(8,128)(2,1)S(1)} collective-permute-done((bf16[256,256]{1,0:T(8,128)(2,1)S(1)}, bf16[256,256]{1,0:T(8,128)(2,1)S(1)}, u32[]{:S(2)}, u32[]{:S(2)}) %collective-permute-start.8) | collective-permute-done | bytes 131104 | tf_op jit(solution)/shard_map/ppermute | solution.py:303
  46.1 2.9 %collective-permute-start.11 = (bf16[256,256]{1,0:T(8,128)(2,1)S(1)}, bf16[256,256]{1,0:T(8,128)(2,1)S(1)}, u32[]{:S(2)}, u32[]{:S(2)}) collective-permute-start(bf16[256,256]{1,0:T(8,128)(2,1)S(1)} %bitcast.15), channel_id=1, source_target_pairs={{0,192},{32,224},{64,0},{96,32},{128,64},{160,96},{192,128},{224,1... | collective-permute-start | bytes 393224 | tf_op jit(solution)/shard_map/ppermute | solution.py:303
  49.0 0.7 collective-permute-start.10
  49.8 9.5 %attend_first.1 = (f32[8,128,512]{2,1,0:T(8,128)S(1)}, f32[256,256]{1,0:T(8,128)S(1)}, bf16[256,256]{1,0:T(8,128)(2,1)S(1)}, bf16[256,256]{1,0:T(8,128)(2,1)S(1)...) custom-call(s32[64]{0:T(128)S(1)} %copy-done.4, ...), custom_call_target="tpu_custom_call" | custom-call | tf_op jit(solution)/shard_map/attend_first/pallas_call | solution.py:191
  59.4 7.4 %attend_second.1 = (f32[8,128,512]{2,1,0:T(8,128)S(1)}, bf16[256,256]{1,0:T(8,128)(2,1)S(1)}, bf16[256,256]{1,0:T(8,128)(2,1)S(1)}, bf16[256,256]{1,0:T(8,128)(2,1)S(1)}, bf16[256,256]{1,0:T(8,128)(2,1)S(1)}) custom-call(s32[64]{0:T(128)S(1)} %copy-done.4, s32[8]{0:T(128)S(1)} %convert_reduce_fusion.sd, s32[64,64]{1,0:T(8,128)S(1)} %multiply_add_fusion.code, ...), custom_call_target="tpu_custom_call" | custom-call | tf_op jit(solution)/shard_map/attend_second/pallas_call | solution.py:191
  66.8 0.1 slice.17
  66.9 0.1 collective-permute-start.14
  67.0 2.1 %collective-permute-start.19 = (bf16[256,256]{1,0:T(8,128)(2,1)S(1)}, bf16[256,256]{1,0:T(8,128)(2,1)S(1)}, u32[]{:S(2)}, u32[]{:S(2)}) collective-permute-start(bf16[256,256]{1,0:T(8,128)(2,1)S(1)} %get-tuple-element.29), channel_id=1, source_target_pairs={{0,192},{32,224},{64,0},{96,32},{128,64},{160,96},{192,128},{224,1... | collective-permute-start | bytes 393224 | tf_op jit(solution)/shard_map/ppermute | solution.py:333
  69.1 0.9 collective-permute-start.20
  70.0 6.5 %collective-permute-start.21 = (bf16[256,256]{1,0:T(8,128)(2,1)S(1)}, bf16[256,256]{1,0:T(8,128)(2,1)S(1)}, u32[]{:S(2)}, u32[]{:S(2)}) collective-permute-start(bf16[256,256]{1,0:T(8,128)(2,1)S(1)} %get-tuple-element.31), channel_id=1, source_target_pairs={{0,224},{32,0},{64,32},{96,64},{128,96},{160,128},{192,160},{224,1... | collective-permute-start | bytes 393224 | tf_op jit(solution)/shard_map/ppermute | solution.py:333
  76.5 1.8 %collective-permute-start.17 = (bf16[256,256]{1,0:T(8,128)(2,1)S(1)}, bf16[256,256]{1,0:T(8,128)(2,1)S(1)}, u32[]{:S(2)}, u32[]{:S(2)}) collective-permute-start(bf16[256,256]{1,0:T(8,128)(2,1)S(1)} %get-tuple-element.27), channel_id=1, source_target_pairs={{0,160},{32,192},{64,224},{96,0},{128,32},{160,64},{192,96},{224,1... | collective-permute-start | bytes 393224 | tf_op jit(solution)/shard_map/ppermute | solution.py:327
  78.3 0.8 fusion
  79.1 2.0 %collective-permute-start.18 = (bf16[256,256]{1,0:T(8,128)(2,1)S(1)}, bf16[256,256]{1,0:T(8,128)(2,1)S(1)}, u32[]{:S(2)}, u32[]{:S(2)}) collective-permute-start(bf16[256,256]{1,0:T(8,128)(2,1)S(1)} %get-tuple-element.28), channel_id=1, source_target_pairs={{0,96},{32,128},{64,160},{96,192},{128,224},{160,0},{192,32},{224,... | collective-permute-start | bytes 393224 | tf_op jit(solution)/shard_map/ppermute | solution.py:327
  81.1 10.0 %collective-permute-start.22 = (bf16[256,256]{1,0:T(8,128)(2,1)S(1)}, bf16[256,256]{1,0:T(8,128)(2,1)S(1)}, u32[]{:S(2)}, u32[]{:S(2)}) collective-permute-start(bf16[256,256]{1,0:T(8,128)(2,1)S(1)} %get-tuple-element.32), channel_id=1, source_target_pairs={{0,32},{32,64},{64,96},{96,128},{128,160},{160,192},{192,224},{224... | collective-permute-start | bytes 393224 | tf_op jit(solution)/shard_map/ppermute | solution.py:333
  91.1 0.7 collective-permute-start.15
  91.8 2.5 %collective-permute-done.17 = bf16[256,256]{1,0:T(8,128)(2,1)S(1)} collective-permute-done((bf16[256,256]{1,0:T(8,128)(2,1)S(1)}, bf16[256,256]{1,0:T(8,128)(2,1)S(1)}, u32[]{:S(2)}, u32[]{:S(2)}) %collective-permute-start.17) | collective-permute-done | bytes 131104 | tf_op jit(solution)/shard_map/ppermute | solution.py:327
  94.3 1.4 %collective-permute-done.18 = bf16[256,256]{1,0:T(8,128)(2,1)S(1)} collective-permute-done((bf16[256,256]{1,0:T(8,128)(2,1)S(1)}, bf16[256,256]{1,0:T(8,128)(2,1)S(1)}, u32[]{:S(2)}, u32[]{:S(2)}) %collective-permute-start.18) | collective-permute-done | bytes 131104 | tf_op jit(solution)/shard_map/ppermute | solution.py:327
  95.6 2.0 %collective-permute-done.22 = bf16[256,256]{1,0:T(8,128)(2,1)S(1)} collective-permute-done((bf16[256,256]{1,0:T(8,128)(2,1)S(1)}, bf16[256,256]{1,0:T(8,128)(2,1)S(1)}, u32[]{:S(2)}, u32[]{:S(2)}) %collective-permute-start.22) | collective-permute-done | bytes 131104 | tf_op jit(solution)/shard_map/ppermute | solution.py:333
  97.6 0.8 convert_add_fusion
  98.5 7.2 %all-to-all-start.1 = ((f32[16,16,256]{2,1,0:T(8,128)}), f32[16,16,256]{2,1,0:T(8,128)S(1)}, u32[]{:S(2)}, u32[]{:S(2)}) async-start(f32[16,16,256]{2,1,0:T(8,128)} %bitcast.18), calls=%async_computation.1 | async-start | bytes 524288 | tf_op jit(solution)/shard_map/all_to_all | solution.py:340
  105.7 2.0 %flip.1 = f32[512,256]{1,0:T(8,128)} custom-call(f32[8,128,512]{2,1,0:T(8,128)S(1)} %get-tuple-element.22.dq, f32[4,128,512]{2,1,0:T(8,128)S(1)} %collective-permute-done.14.other, bf16[4,128,256]{2,1,0:T(8,128)(2,1)} %collective-permute-done.15.mate), custom_call_target="tpu_custom_call" | custom-call | tf_op jit(solution)/shard_map/flip/pallas_call | solution.py:236
  107.7 5.0 %all-to-all-done.1.parts = f32[16,16,256]{2,1,0:T(8,128)S(1)} async-done(((f32[16,16,256]{2,1,0:T(8,128)}), f32[16,16,256]{2,1,0:T(8,128)S(1)}, u32[]{:S(2)}, u32[]{:S(2)}) %all-to-all-start.1) | async-done | bytes 262176 | tf_op jit(solution)/shard_map/all_to_all | solution.py:340
  112.7 0.7 unpack.1
  (37 shorter events, 0.1 us)
Async XLA Ops:
  1.6 16.1 %copy-start.7 = (f32[2,512]{1,0:T(2,128)S(1)}, f32[2,512]{1,0:T(2,128)}, u32[]{:S(2)}) copy-start(f32[2,512]{1,0:T(2,128)} %param.14) | copy-start | bytes 12292
  1.6 31.4 %copy-start.6 = (s32[8192]{0:T(1024)S(1)}, s32[8192]{0:T(1024)}, u32[]{:S(2)}) copy-start(s32[8192]{0:T(1024)} %param.16) | copy-start | bytes 98308
  1.6 48.2 %copy-start.5 = (s32[2,64,64]{2,1,0:T(8,128)S(1)}, s32[2,64,64]{2,1,0:T(8,128)}, u32[]{:S(2)}) copy-start(s32[2,64,64]{2,1,0:T(8,128)} %param.15) | copy-start | bytes 98308
  1.6 48.2 %copy-start.4 = (s32[64]{0:T(128)S(1)}, s32[64]{0:T(128)}, u32[]{:S(2)}) copy-start(s32[64]{0:T(128)} %bo.3) | copy-start | bytes 772
  2.7 47.2 %copy-start = (bf16[512,256]{1,0:T(8,128)(2,1)S(1)}, bf16[512,256]{1,0:T(8,128)(2,1)}, u32[]{:S(2)}) copy-start(bf16[512,256]{1,0:T(8,128)(2,1)} %refs_1_.1) | copy-start | bytes 786436
  2.7 47.2 %copy-start.1 = (bf16[512,256]{1,0:T(8,128)(2,1)S(1)}, bf16[512,256]{1,0:T(8,128)(2,1)}, u32[]{:S(2)}) copy-start(bf16[512,256]{1,0:T(8,128)(2,1)} %refs_0_.1) | copy-start | bytes 786436
  2.7 14.9 %collective-permute-start.2 = (bf16[512,512]{1,0:T(8,128)(2,1)S(1)}, bf16[512,512]{1,0:T(8,128)(2,1)S(1)}, u32[]{:S(2)}, u32[]{:S(2)}) collective-permute-start(bf16[512,512]{1,0:T(8,128)(2,1)S(1)} %constant_dynamic-update-slice_fusion), channel_id=1, source_target_pairs={{0,1},{1,0},{2,3},{3,2},{4,5},{5,4},{6,7},{7,6},{8,9},{9,8},{10,11... | collective-permute-start | bytes 1572872 | tf_op jit(solution)/shard_map/ppermute | solution.py:306
  4.9 44.1 %collective-permute-start.1 = (bf16[512,512]{1,0:T(8,128)(2,1)S(1)}, bf16[512,512]{1,0:T(8,128)(2,1)S(1)}, u32[]{:S(2)}, u32[]{:S(2)}) collective-permute-start(bf16[512,512]{1,0:T(8,128)(2,1)S(1)} %constant_dynamic-update-slice_fusion), channel_id=1, source_target_pairs={{0,16},{16,0},{1,17},{17,1},{2,18},{18,2},{3,19},{19,3},{4,20},{20... | collective-permute-start | bytes 1572872 | tf_op jit(solution)/shard_map/ppermute | solution.py:307
  5.7 22.9 %collective-permute-start = (s32[64,64]{1,0:T(8,128)S(1)}, s32[64,64]{1,0:T(8,128)S(1)}, u32[]{:S(2)}, u32[]{:S(2)}) collective-permute-start(s32[64,64]{1,0:T(8,128)S(1)} %add_bitcast_fusion), channel_id=1, source_target_pairs={{0,1},{1,0},{2,3},{3,2},{4,5},{5,4},{6,7},{7,6},{8,9},{9,8},{10,11... | collective-permute-start | bytes 49160 | tf_op jit(solution)/shard_map/ppermute | solution.py:317
  5.8 0.8 copy-start.2
  6.7 0.8 copy-start.3
  8.3 13.6 %all-to-all-start = ((bf16[16,16,256]{2,1,0:T(8,128)(2,1)}), bf16[16,16,256]{2,1,0:T(8,128)(2,1)S(1)}, u32[]{:S(2)}, u32[]{:S(2)}) async-start(bf16[16,16,256]{2,1,0:T(8,128)(2,1)} %pack.1), calls=%async_computation | async-start | bytes 262144 | tf_op jit(solution)/shard_map/all_to_all | solution.py:300
  17.6 32.2 %collective-permute-start.3 = (bf16[512,512]{1,0:T(8,128)(2,1)S(1)}, bf16[512,512]{1,0:T(8,128)(2,1)S(1)}, u32[]{:S(2)}, u32[]{:S(2)}) collective-permute-start(bf16[512,512]{1,0:T(8,128)(2,1)S(1)} %collective-permute-done.2.refs_3_), channel_id=1, source_target_pairs={{0,16},{16,0},{1,17},{17,1},{2,18},{18,2},{3,19},{19,3},{4,20},{20... | collective-permute-start | bytes 1572872 | tf_op jit(solution)/shard_map/ppermute | solution.py:308
  17.7 3.7 %collective-permute-start.5 = (f32[4,512]{1,0:T(4,128)S(1)}, f32[4,512]{1,0:T(4,128)S(1)}, u32[]{:S(2)}, u32[]{:S(2)}) collective-permute-start(f32[4,512]{1,0:T(4,128)S(1)} %pad_maximum_fusion.refs_5_.refs_3_), channel_id=1, source_target_pairs={{0,1},{1,0},{2,3},{3,2},{4,5},{5,4},{6,7},{7,6},{8,9},{9,8},{10,11... | collective-permute-start | bytes 24584 | tf_op jit(solution)/shard_map/ppermute | solution.py:313
  17.9 3.6 %collective-permute-start.4 = (f32[4,512]{1,0:T(4,128)S(1)}, f32[4,512]{1,0:T(4,128)S(1)}, u32[]{:S(2)}, u32[]{:S(2)}) collective-permute-start(f32[4,512]{1,0:T(4,128)S(1)} %pad_maximum_fusion.refs_5_.refs_3_), channel_id=1, source_target_pairs={{0,16},{16,0},{1,17},{17,1},{2,18},{18,2},{3,19},{19,3},{4,20},{20... | collective-permute-start | bytes 24584 | tf_op jit(solution)/shard_map/ppermute | solution.py:314
  21.4 7.2 %collective-permute-start.6 = (f32[4,512]{1,0:T(4,128)S(1)}, f32[4,512]{1,0:T(4,128)S(1)}, u32[]{:S(2)}, u32[]{:S(2)}) collective-permute-start(f32[4,512]{1,0:T(4,128)S(1)} %collective-permute-done.5.refs_7_.refs_5_), channel_id=1, source_target_pairs={{0,16},{16,0},{1,17},{17,1},{2,18},{18,2},{3,19},{19,3},{4,20},{20... | collective-permute-start | bytes 24584 | tf_op jit(solution)/shard_map/ppermute | solution.py:315
  21.9 21.0 %collective-permute-start.9 = (bf16[256,256]{1,0:T(8,128)(2,1)S(1)}, bf16[256,256]{1,0:T(8,128)(2,1)S(1)}, u32[]{:S(2)}, u32[]{:S(2)}) collective-permute-start(bf16[256,256]{1,0:T(8,128)(2,1)S(1)} %bitcast.10), channel_id=1, source_target_pairs={{0,160},{32,192},{64,224},{96,0},{128,32},{160,64},{192,96},{224,1... | collective-permute-start | bytes 393224 | tf_op jit(solution)/shard_map/ppermute | solution.py:303
  28.6 17.5 %collective-permute-start.8 = (bf16[256,256]{1,0:T(8,128)(2,1)S(1)}, bf16[256,256]{1,0:T(8,128)(2,1)S(1)}, u32[]{:S(2)}, u32[]{:S(2)}) collective-permute-start(bf16[256,256]{1,0:T(8,128)(2,1)S(1)} %bitcast.11), channel_id=1, source_target_pairs={{0,96},{32,128},{64,160},{96,192},{128,224},{160,0},{192,32},{224,... | collective-permute-start | bytes 393224 | tf_op jit(solution)/shard_map/ppermute | solution.py:303
  28.7 17.5 %collective-permute-start.7 = (bf16[256,256]{1,0:T(8,128)(2,1)S(1)}, bf16[256,256]{1,0:T(8,128)(2,1)S(1)}, u32[]{:S(2)}, u32[]{:S(2)}) collective-permute-start(bf16[256,256]{1,0:T(8,128)(2,1)S(1)} %bitcast.12), channel_id=1, source_target_pairs={{0,128},{32,160},{64,192},{96,224},{128,0},{160,32},{192,64},{224,... | collective-permute-start | bytes 393224 | tf_op jit(solution)/shard_map/ppermute | solution.py:303
  42.9 16.5 %collective-permute-start.13 = (bf16[256,256]{1,0:T(8,128)(2,1)S(1)}, bf16[256,256]{1,0:T(8,128)(2,1)S(1)}, u32[]{:S(2)}, u32[]{:S(2)}) collective-permute-start(bf16[256,256]{1,0:T(8,128)(2,1)S(1)} %bitcast.13), channel_id=1, source_target_pairs={{0,224},{32,0},{64,32},{96,64},{128,96},{160,128},{192,160},{224,1... | collective-permute-start | bytes 393224 | tf_op jit(solution)/shard_map/ppermute | solution.py:303
  46.1 13.3 %collective-permute-start.12 = (bf16[256,256]{1,0:T(8,128)(2,1)S(1)}, bf16[256,256]{1,0:T(8,128)(2,1)S(1)}, u32[]{:S(2)}, u32[]{:S(2)}) collective-permute-start(bf16[256,256]{1,0:T(8,128)(2,1)S(1)} %bitcast.14), channel_id=1, source_target_pairs={{0,32},{32,64},{64,96},{96,128},{128,160},{160,192},{192,224},{224... | collective-permute-start | bytes 393224 | tf_op jit(solution)/shard_map/ppermute | solution.py:303
  46.1 13.3 %collective-permute-start.11 = (bf16[256,256]{1,0:T(8,128)(2,1)S(1)}, bf16[256,256]{1,0:T(8,128)(2,1)S(1)}, u32[]{:S(2)}, u32[]{:S(2)}) collective-permute-start(bf16[256,256]{1,0:T(8,128)(2,1)S(1)} %bitcast.15), channel_id=1, source_target_pairs={{0,192},{32,224},{64,0},{96,32},{128,64},{160,96},{192,128},{224,1... | collective-permute-start | bytes 393224 | tf_op jit(solution)/shard_map/ppermute | solution.py:303
  49.0 10.4 %collective-permute-start.10 = (bf16[256,256]{1,0:T(8,128)(2,1)S(1)}, bf16[256,256]{1,0:T(8,128)(2,1)S(1)}, u32[]{:S(2)}, u32[]{:S(2)}) collective-permute-start(bf16[256,256]{1,0:T(8,128)(2,1)S(1)} %bitcast.16), channel_id=1, source_target_pairs={{0,64},{32,96},{64,128},{96,160},{128,192},{160,224},{192,0},{224,... | collective-permute-start | bytes 393224 | tf_op jit(solution)/shard_map/ppermute | solution.py:303
  66.9 9.6 %collective-permute-start.14 = (f32[4,128,512]{2,1,0:T(8,128)S(1)}, f32[4,128,512]{2,1,0:T(8,128)S(1)}, u32[]{:S(2)}, u32[]{:S(2)}) collective-permute-start(f32[4,128,512]{2,1,0:T(8,128)S(1)} %slice.17), channel_id=1, source_target_pairs={{0,16},{16,0},{1,17},{17,1},{2,18},{18,2},{3,19},{19,3},{4,20},{20... | collective-permute-start | bytes 3145736 | tf_op jit(solution)/shard_map/ppermute | solution.py:329
  67.0 12.1 %collective-permute-start.19 = (bf16[256,256]{1,0:T(8,128)(2,1)S(1)}, bf16[256,256]{1,0:T(8,128)(2,1)S(1)}, u32[]{:S(2)}, u32[]{:S(2)}) collective-permute-start(bf16[256,256]{1,0:T(8,128)(2,1)S(1)} %get-tuple-element.29), channel_id=1, source_target_pairs={{0,192},{32,224},{64,0},{96,32},{128,64},{160,96},{192,128},{224,1... | collective-permute-start | bytes 393224 | tf_op jit(solution)/shard_map/ppermute | solution.py:333
  69.1 12.1 %collective-permute-start.20 = (bf16[256,256]{1,0:T(8,128)(2,1)S(1)}, bf16[256,256]{1,0:T(8,128)(2,1)S(1)}, u32[]{:S(2)}, u32[]{:S(2)}) collective-permute-start(bf16[256,256]{1,0:T(8,128)(2,1)S(1)} %get-tuple-element.30), channel_id=1, source_target_pairs={{0,64},{32,96},{64,128},{96,160},{128,192},{160,224},{192,0},{224,... | collective-permute-start | bytes 393224 | tf_op jit(solution)/shard_map/ppermute | solution.py:333
  70.0 21.1 %collective-permute-start.21 = (bf16[256,256]{1,0:T(8,128)(2,1)S(1)}, bf16[256,256]{1,0:T(8,128)(2,1)S(1)}, u32[]{:S(2)}, u32[]{:S(2)}) collective-permute-start(bf16[256,256]{1,0:T(8,128)(2,1)S(1)} %get-tuple-element.31), channel_id=1, source_target_pairs={{0,224},{32,0},{64,32},{96,64},{128,96},{160,128},{192,160},{224,1... | collective-permute-start | bytes 393224 | tf_op jit(solution)/shard_map/ppermute | solution.py:333
  76.5 15.3 %collective-permute-start.16 = (bf16[256,256]{1,0:T(8,128)(2,1)S(1)}, bf16[256,256]{1,0:T(8,128)(2,1)S(1)}, u32[]{:S(2)}, u32[]{:S(2)}) collective-permute-start(bf16[256,256]{1,0:T(8,128)(2,1)S(1)} %get-tuple-element.26), channel_id=1, source_target_pairs={{0,128},{32,160},{64,192},{96,224},{128,0},{160,32},{192,64},{224,... | collective-permute-start | bytes 393224 | tf_op jit(solution)/shard_map/ppermute | solution.py:327
  76.5 17.8 %collective-permute-start.17 = (bf16[256,256]{1,0:T(8,128)(2,1)S(1)}, bf16[256,256]{1,0:T(8,128)(2,1)S(1)}, u32[]{:S(2)}, u32[]{:S(2)}) collective-permute-start(bf16[256,256]{1,0:T(8,128)(2,1)S(1)} %get-tuple-element.27), channel_id=1, source_target_pairs={{0,160},{32,192},{64,224},{96,0},{128,32},{160,64},{192,96},{224,1... | collective-permute-start | bytes 393224 | tf_op jit(solution)/shard_map/ppermute | solution.py:327
  79.1 16.6 %collective-permute-start.18 = (bf16[256,256]{1,0:T(8,128)(2,1)S(1)}, bf16[256,256]{1,0:T(8,128)(2,1)S(1)}, u32[]{:S(2)}, u32[]{:S(2)}) collective-permute-start(bf16[256,256]{1,0:T(8,128)(2,1)S(1)} %get-tuple-element.28), channel_id=1, source_target_pairs={{0,96},{32,128},{64,160},{96,192},{128,224},{160,0},{192,32},{224,... | collective-permute-start | bytes 393224 | tf_op jit(solution)/shard_map/ppermute | solution.py:327
  81.1 16.5 %collective-permute-start.22 = (bf16[256,256]{1,0:T(8,128)(2,1)S(1)}, bf16[256,256]{1,0:T(8,128)(2,1)S(1)}, u32[]{:S(2)}, u32[]{:S(2)}) collective-permute-start(bf16[256,256]{1,0:T(8,128)(2,1)S(1)} %get-tuple-element.32), channel_id=1, source_target_pairs={{0,32},{32,64},{64,96},{96,128},{128,160},{160,192},{192,224},{224... | collective-permute-start | bytes 393224 | tf_op jit(solution)/shard_map/ppermute | solution.py:333
  91.1 14.6 %collective-permute-start.15 = (bf16[4,128,256]{2,1,0:T(8,128)(2,1)}, bf16[4,128,256]{2,1,0:T(8,128)(2,1)}, u32[]{:S(2)}, u32[]{:S(2)}) collective-permute-start(bf16[4,128,256]{2,1,0:T(8,128)(2,1)} %fusion), channel_id=1, source_target_pairs={{0,1},{1,0},{2,3},{3,2},{4,5},{5,4},{6,7},{7,6},{8,9},{9,8},{10,11... | collective-permute-start | bytes 786440 | tf_op jit(solution)/shard_map/ppermute | solution.py:334
  98.5 14.2 %all-to-all-start.1 = ((f32[16,16,256]{2,1,0:T(8,128)}), f32[16,16,256]{2,1,0:T(8,128)S(1)}, u32[]{:S(2)}, u32[]{:S(2)}) async-start(f32[16,16,256]{2,1,0:T(8,128)} %bitcast.18), calls=%async_computation.1 | async-start | bytes 524288 | tf_op jit(solution)/shard_map/all_to_all | solution.py:340

commit v2 on v1

--- a/solution.py
+++ b/solution.py
@@ -248,8 +248,8 @@
     for g in range(8):
         for half in range(2):
             r, cols = slice(16 * half, 16 * half + 16), slice(g * D, (g + 1) * D)
-            keys[r, cols] = parts[2 * g + half, :, 0:D]
-            values[r, cols] = parts[2 * g + half, :, D : 2 * D]
+            keys[r, cols] = parts[2 * g + half, :, 0:D].astype(jnp.float32)
+            values[r, cols] = parts[2 * g + half, :, D : 2 * D].astype(jnp.float32)
 
 
 def unpack(parts):
@@ -337,7 +337,7 @@
     total = own
     for kk in INS:
         total = total + back[kk].astype(jnp.float32)
-    out = lax.all_to_all(total.reshape(16, 16, 2 * D), HEAD, 0, 0, tiled=True)
+    out = lax.all_to_all(total.astype(jnp.bfloat16).reshape(16, 16, 2 * D), HEAD, 0, 0, tiled=True)
     key_grad, value_grad = unpack(out)
     return query_grad, key_grad, value_grad
 

time: 114 us -> 114 us (level)
  blocking collectives: 0 us -> 13.4 us
  starting transfers between devices: 56.2 us -> 50.1 us
  waiting for transfers between devices: 27.3 us -> 21.9 us
  other arithmetic: 4.37 us -> 3.04 us
    all_to_all x0 -> x1, blocking collectives: none -> 13.4 us  [body(): lax.all_to_all(total.astype(jnp.bfloat16).reshape(16, 16, 2 * D), HEAD, 0...]
    all_to_all x1 -> x0, starting transfers between devices: 7.21 us -> none  [body(): out = lax.all_to_all(total.reshape(16, 16, 2 * D), HEAD, 0, 0, tiled=True)]
    all_to_all x1 -> x0, waiting for transfers between devices: 4.96 us -> none  [body(): out = lax.all_to_all(total.reshape(16, 16, 2 * D), HEAD, 0, 0, tiled=True)]
  transfers between devices with their start and end apart: 25 -> 24, of which waited for: 8 -> 7; matrix products, arithmetic and copies ran while one was open for 4% -> 3% of each run, Pallas kernels for 11% -> 10%
where the time goes in v2:
time: 114 us; the launch traced here: 113 us
  starting transfers between devices  50.1 us (44%)
  waiting for transfers between devices  21.9 us (19%)
  Pallas kernels  19.5 us (17%)
  blocking collectives  13.4 us (12%)
  local copies, waits for them, and re-layouts  4.14 us (4%)
  other arithmetic  3.04 us (3%)
    ppermute x7, starting transfers between devices, body(): back[kk] = lax.ppermute(part, 'z', turn(-kk))  24.3 us
    pallas_call x2, Pallas kernels, attend(): pl.pallas_call(make_kernel(offsets, first), in_specs=[smem] * 4 + [hbm if...  16.9 us
    ppermute x7, starting transfers between devices, body(): kvs[kk] = lax.ppermute(kv, 'z', turn(kk))  14.7 us
    all_to_all x1, blocking collectives, body(): lax.all_to_all(total.astype(jnp.bfloat16).reshape(16, 16, 2 * D), HEAD, 0...  13.4 us
    ppermute x7, waiting for transfers between devices, body(): kvs[kk] = lax.ppermute(kv, 'z', turn(kk))  13 us
    all_to_all x1, starting transfers between devices, body(): kv = lax.all_to_all(kv, HEAD, 0, 0, tiled=True).reshape(CHUNK, 2 * D)  7.16 us
    ppermute x7, waiting for transfers between devices, body(): back[kk] = lax.ppermute(part, 'z', turn(-kk))  5.39 us
    ppermute x1, waiting for transfers between devices, body(): aux2 = lax.ppermute(aux0, 'p', SWAP)  3.07 us
  transfers between devices with their start and end apart: 24, of which 7 were waited for; matrix products, arithmetic and copies ran while one was open for 3% of the time, Pallas kernels for 10%

profile of v2, /device:TPU:8, one launch (start us, length us, event | category | flops | bytes accessed | tf_op | source)
XLA Modules:
  0.0 112.9 jit_solution(508523563936539556)
XLA Ops:
  0.6 1.0 constant_dynamic-update-slice_fusion.1
  1.6 0.0 copy-start.5
  1.6 0.0 copy-start.4
  1.7 1.0 constant_dynamic-update-slice_fusion
  2.7 0.0 copy-start.1
  2.7 2.2 %collective-permute-start.2 = (bf16[512,512]{1,0:T(8,128)(2,1)S(1)}, bf16[512,512]{1,0:T(8,128)(2,1)S(1)}, u32[]{:S(2)}, u32[]{:S(2)}) collective-permute-start(bf16[512,512]{1,0:T(8,128)(2,1)S(1)} %constant_dynamic-update-slice_fusion), channel_id=1, source_target_pairs={{0,1},{1,0},{2,3},{3,2},{4,5},{5,4},{6,7},{7,6},{8,9},{9,8},{10,11... | collective-permute-start | bytes 1572872 | tf_op jit(solution)/shard_map/ppermute | solution.py:306
  4.9 0.8 add_bitcast_fusion
  5.7 0.1 collective-permute-start
  5.8 0.8 copy-done.2
  6.7 0.8 copy-done.3
  7.5 0.8 pack.1
  8.3 7.2 %all-to-all-start = ((bf16[16,16,256]{2,1,0:T(8,128)(2,1)}), bf16[16,16,256]{2,1,0:T(8,128)(2,1)S(1)}, u32[]{:S(2)}, u32[]{:S(2)}) async-start(bf16[16,16,256]{2,1,0:T(8,128)(2,1)} %pack.1), calls=%async_computation | async-start | bytes 262144 | tf_op jit(solution)/shard_map/all_to_all | solution.py:300
  15.5 1.1 convert_multiply_fusion
  16.6 0.3 reshape.19
  16.9 0.6 reduce_sum.19
  17.5 0.1 copy.13
  17.6 0.1 collective-permute-start.3
  17.7 0.2 collective-permute-start.5
  17.9 0.5 collective-permute-start.4
  18.4 3.1 %collective-permute-done.5.refs_7_.refs_5_ = f32[4,512]{1,0:T(4,128)S(1)} collective-permute-done((f32[4,512]{1,0:T(4,128)S(1)}, f32[4,512]{1,0:T(4,128)S(1)}, u32[]{:S(2)}, u32[]{:S(2)}) %collective-permute-start.5) | collective-permute-done | bytes 8224 | tf_op jit(solution)/shard_map/ppermute | solution.py:313
  21.4 0.5 all-to-all-done
  21.9 6.7 %collective-permute-start.9 = (bf16[256,256]{1,0:T(8,128)(2,1)S(1)}, bf16[256,256]{1,0:T(8,128)(2,1)S(1)}, u32[]{:S(2)}, u32[]{:S(2)}) collective-permute-start(bf16[256,256]{1,0:T(8,128)(2,1)S(1)} %bitcast.10), channel_id=1, source_target_pairs={{0,160},{32,192},{64,224},{96,0},{128,32},{160,64},{192,96},{224,1... | collective-permute-start | bytes 393224 | tf_op jit(solution)/shard_map/ppermute | solution.py:303
  28.7 4.3 %collective-permute-start.7 = (bf16[256,256]{1,0:T(8,128)(2,1)S(1)}, bf16[256,256]{1,0:T(8,128)(2,1)S(1)}, u32[]{:S(2)}, u32[]{:S(2)}) collective-permute-start(bf16[256,256]{1,0:T(8,128)(2,1)S(1)} %bitcast.12), channel_id=1, source_target_pairs={{0,128},{32,160},{64,192},{96,224},{128,0},{160,32},{192,64},{224,... | collective-permute-start | bytes 393224 | tf_op jit(solution)/shard_map/ppermute | solution.py:303
  32.9 0.1 pad_add_fusion.meta
  33.0 0.2 convert_reduce_fusion.sd
  33.2 9.7 %collective-permute-done.9.refs_12_ = bf16[256,256]{1,0:T(8,128)(2,1)S(1)} collective-permute-done((bf16[256,256]{1,0:T(8,128)(2,1)S(1)}, bf16[256,256]{1,0:T(8,128)(2,1)S(1)}, u32[]{:S(2)}, u32[]{:S(2)}) %collective-permute-start.9) | collective-permute-done | bytes 131104 | tf_op jit(solution)/shard_map/ppermute | solution.py:303
  42.9 3.3 %collective-permute-done.8.refs_11_ = bf16[256,256]{1,0:T(8,128)(2,1)S(1)} collective-permute-done((bf16[256,256]{1,0:T(8,128)(2,1)S(1)}, bf16[256,256]{1,0:T(8,128)(2,1)S(1)}, u32[]{:S(2)}, u32[]{:S(2)}) %collective-permute-start.8) | collective-permute-done | bytes 131104 | tf_op jit(solution)/shard_map/ppermute | solution.py:303
  46.1 2.9 %collective-permute-start.11 = (bf16[256,256]{1,0:T(8,128)(2,1)S(1)}, bf16[256,256]{1,0:T(8,128)(2,1)S(1)}, u32[]{:S(2)}, u32[]{:S(2)}) collective-permute-start(bf16[256,256]{1,0:T(8,128)(2,1)S(1)} %bitcast.15), channel_id=1, source_target_pairs={{0,192},{32,224},{64,0},{96,32},{128,64},{160,96},{192,128},{224,1... | collective-permute-start | bytes 393224 | tf_op jit(solution)/shard_map/ppermute | solution.py:303
  49.0 0.7 collective-permute-start.10
  49.8 9.5 %attend_first.1 = (f32[8,128,512]{2,1,0:T(8,128)S(1)}, f32[256,256]{1,0:T(8,128)S(1)}, bf16[256,256]{1,0:T(8,128)(2,1)S(1)}, bf16[256,256]{1,0:T(8,128)(2,1)S(1)...) custom-call(s32[64]{0:T(128)S(1)} %copy-done.4, ...), custom_call_target="tpu_custom_call" | custom-call | tf_op jit(solution)/shard_map/attend_first/pallas_call | solution.py:191
  59.4 7.4 %attend_second.1 = (f32[8,128,512]{2,1,0:T(8,128)S(1)}, bf16[256,256]{1,0:T(8,128)(2,1)S(1)}, bf16[256,256]{1,0:T(8,128)(2,1)S(1)}, bf16[256,256]{1,0:T(8,128)(2,1)S(1)}, bf16[256,256]{1,0:T(8,128)(2,1)S(1)}) custom-call(s32[64]{0:T(128)S(1)} %copy-done.4, s32[8]{0:T(128)S(1)} %convert_reduce_fusion.sd, s32[64,64]{1,0:T(8,128)S(1)} %multiply_add_fusion.code, ...), custom_call_target="tpu_custom_call" | custom-call | tf_op jit(solution)/shard_map/attend_second/pallas_call | solution.py:191
  66.8 0.1 slice.17
  66.9 0.1 collective-permute-start.14
  67.0 2.1 %collective-permute-start.19 = (bf16[256,256]{1,0:T(8,128)(2,1)S(1)}, bf16[256,256]{1,0:T(8,128)(2,1)S(1)}, u32[]{:S(2)}, u32[]{:S(2)}) collective-permute-start(bf16[256,256]{1,0:T(8,128)(2,1)S(1)} %get-tuple-element.29), channel_id=1, source_target_pairs={{0,192},{32,224},{64,0},{96,32},{128,64},{160,96},{192,128},{224,1... | collective-permute-start | bytes 393224 | tf_op jit(solution)/shard_map/ppermute | solution.py:333
  69.1 0.9 collective-permute-start.20
  70.0 6.5 %collective-permute-start.21 = (bf16[256,256]{1,0:T(8,128)(2,1)S(1)}, bf16[256,256]{1,0:T(8,128)(2,1)S(1)}, u32[]{:S(2)}, u32[]{:S(2)}) collective-permute-start(bf16[256,256]{1,0:T(8,128)(2,1)S(1)} %get-tuple-element.31), channel_id=1, source_target_pairs={{0,224},{32,0},{64,32},{96,64},{128,96},{160,128},{192,160},{224,1... | collective-permute-start | bytes 393224 | tf_op jit(solution)/shard_map/ppermute | solution.py:333
  76.5 1.8 %collective-permute-start.17 = (bf16[256,256]{1,0:T(8,128)(2,1)S(1)}, bf16[256,256]{1,0:T(8,128)(2,1)S(1)}, u32[]{:S(2)}, u32[]{:S(2)}) collective-permute-start(bf16[256,256]{1,0:T(8,128)(2,1)S(1)} %get-tuple-element.27), channel_id=1, source_target_pairs={{0,160},{32,192},{64,224},{96,0},{128,32},{160,64},{192,96},{224,1... | collective-permute-start | bytes 393224 | tf_op jit(solution)/shard_map/ppermute | solution.py:327
  78.3 0.1 fusion
  78.4 2.1 %collective-permute-start.18 = (bf16[256,256]{1,0:T(8,128)(2,1)S(1)}, bf16[256,256]{1,0:T(8,128)(2,1)S(1)}, u32[]{:S(2)}, u32[]{:S(2)}) collective-permute-start(bf16[256,256]{1,0:T(8,128)(2,1)S(1)} %get-tuple-element.28), channel_id=1, source_target_pairs={{0,96},{32,128},{64,160},{96,192},{128,224},{160,0},{192,32},{224,... | collective-permute-start | bytes 393224 | tf_op jit(solution)/shard_map/ppermute | solution.py:327
  80.6 10.9 %collective-permute-start.22 = (bf16[256,256]{1,0:T(8,128)(2,1)S(1)}, bf16[256,256]{1,0:T(8,128)(2,1)S(1)}, u32[]{:S(2)}, u32[]{:S(2)}) collective-permute-start(bf16[256,256]{1,0:T(8,128)(2,1)S(1)} %get-tuple-element.32), channel_id=1, source_target_pairs={{0,32},{32,64},{64,96},{96,128},{128,160},{160,192},{192,224},{224... | collective-permute-start | bytes 393224 | tf_op jit(solution)/shard_map/ppermute | solution.py:333
  91.5 0.8 collective-permute-start.15
  92.3 2.1 %collective-permute-done.17 = bf16[256,256]{1,0:T(8,128)(2,1)S(1)} collective-permute-done((bf16[256,256]{1,0:T(8,128)(2,1)S(1)}, bf16[256,256]{1,0:T(8,128)(2,1)S(1)}, u32[]{:S(2)}, u32[]{:S(2)}) %collective-permute-start.17) | collective-permute-done | bytes 131104 | tf_op jit(solution)/shard_map/ppermute | solution.py:327
  94.4 1.1 collective-permute-done.18
  95.4 2.2 %collective-permute-done.22 = bf16[256,256]{1,0:T(8,128)(2,1)S(1)} collective-permute-done((bf16[256,256]{1,0:T(8,128)(2,1)S(1)}, bf16[256,256]{1,0:T(8,128)(2,1)S(1)}, u32[]{:S(2)}, u32[]{:S(2)}) %collective-permute-start.22) | collective-permute-done | bytes 131104 | tf_op jit(solution)/shard_map/ppermute | solution.py:333
  97.6 0.2 add_convert_fusion
  97.8 13.4 %all_to_all.10.parts = bf16[16,16,256]{2,1,0:T(8,128)(2,1)S(1)} all-to-all(bf16[16,16,256]{2,1,0:T(8,128)(2,1)S(1)} %bitcast.18), channel_id=1, replica_groups=mesh['z'=8,'c'=2,'x'=4,'w'=2,'p'=2] {'x','w','p'}, dimensions={0} | all-to-all | bytes 262144 | tf_op jit(solution)/shard_map/all_to_all | solution.py:340
  111.2 0.7 unpack.1
  111.9 1.0 flip.1
  (36 shorter events, 0.1 us)
Async XLA Ops:
  1.6 16.1 %copy-start.7 = (f32[2,512]{1,0:T(2,128)S(1)}, f32[2,512]{1,0:T(2,128)}, u32[]{:S(2)}) copy-start(f32[2,512]{1,0:T(2,128)} %param.14) | copy-start | bytes 12292
  1.6 31.4 %copy-start.6 = (s32[8192]{0:T(1024)S(1)}, s32[8192]{0:T(1024)}, u32[]{:S(2)}) copy-start(s32[8192]{0:T(1024)} %param.16) | copy-start | bytes 98308
  1.6 48.2 %copy-start.5 = (s32[2,64,64]{2,1,0:T(8,128)S(1)}, s32[2,64,64]{2,1,0:T(8,128)}, u32[]{:S(2)}) copy-start(s32[2,64,64]{2,1,0:T(8,128)} %param.15) | copy-start | bytes 98308
  1.6 48.2 %copy-start.4 = (s32[64]{0:T(128)S(1)}, s32[64]{0:T(128)}, u32[]{:S(2)}) copy-start(s32[64]{0:T(128)} %bo.3) | copy-start | bytes 772
  2.7 47.2 %copy-start = (bf16[512,256]{1,0:T(8,128)(2,1)S(1)}, bf16[512,256]{1,0:T(8,128)(2,1)}, u32[]{:S(2)}) copy-start(bf16[512,256]{1,0:T(8,128)(2,1)} %refs_1_.1) | copy-start | bytes 786436
  2.7 47.2 %copy-start.1 = (bf16[512,256]{1,0:T(8,128)(2,1)S(1)}, bf16[512,256]{1,0:T(8,128)(2,1)}, u32[]{:S(2)}) copy-start(bf16[512,256]{1,0:T(8,128)(2,1)} %refs_0_.1) | copy-start | bytes 786436
  2.7 14.9 %collective-permute-start.2 = (bf16[512,512]{1,0:T(8,128)(2,1)S(1)}, bf16[512,512]{1,0:T(8,128)(2,1)S(1)}, u32[]{:S(2)}, u32[]{:S(2)}) collective-permute-start(bf16[512,512]{1,0:T(8,128)(2,1)S(1)} %constant_dynamic-update-slice_fusion), channel_id=1, source_target_pairs={{0,1},{1,0},{2,3},{3,2},{4,5},{5,4},{6,7},{7,6},{8,9},{9,8},{10,11... | collective-permute-start | bytes 1572872 | tf_op jit(solution)/shard_map/ppermute | solution.py:306
  4.9 44.1 %collective-permute-start.1 = (bf16[512,512]{1,0:T(8,128)(2,1)S(1)}, bf16[512,512]{1,0:T(8,128)(2,1)S(1)}, u32[]{:S(2)}, u32[]{:S(2)}) collective-permute-start(bf16[512,512]{1,0:T(8,128)(2,1)S(1)} %constant_dynamic-update-slice_fusion), channel_id=1, source_target_pairs={{0,16},{16,0},{1,17},{17,1},{2,18},{18,2},{3,19},{19,3},{4,20},{20... | collective-permute-start | bytes 1572872 | tf_op jit(solution)/shard_map/ppermute | solution.py:307
  5.7 22.9 %collective-permute-start = (s32[64,64]{1,0:T(8,128)S(1)}, s32[64,64]{1,0:T(8,128)S(1)}, u32[]{:S(2)}, u32[]{:S(2)}) collective-permute-start(s32[64,64]{1,0:T(8,128)S(1)} %add_bitcast_fusion), channel_id=1, source_target_pairs={{0,1},{1,0},{2,3},{3,2},{4,5},{5,4},{6,7},{7,6},{8,9},{9,8},{10,11... | collective-permute-start | bytes 49160 | tf_op jit(solution)/shard_map/ppermute | solution.py:317
  5.8 0.8 copy-start.2
  6.7 0.8 copy-start.3
  8.3 13.6 %all-to-all-start = ((bf16[16,16,256]{2,1,0:T(8,128)(2,1)}), bf16[16,16,256]{2,1,0:T(8,128)(2,1)S(1)}, u32[]{:S(2)}, u32[]{:S(2)}) async-start(bf16[16,16,256]{2,1,0:T(8,128)(2,1)} %pack.1), calls=%async_computation | async-start | bytes 262144 | tf_op jit(solution)/shard_map/all_to_all | solution.py:300
  17.6 32.2 %collective-permute-start.3 = (bf16[512,512]{1,0:T(8,128)(2,1)S(1)}, bf16[512,512]{1,0:T(8,128)(2,1)S(1)}, u32[]{:S(2)}, u32[]{:S(2)}) collective-permute-start(bf16[512,512]{1,0:T(8,128)(2,1)S(1)} %collective-permute-done.2.refs_3_), channel_id=1, source_target_pairs={{0,16},{16,0},{1,17},{17,1},{2,18},{18,2},{3,19},{19,3},{4,20},{20... | collective-permute-start | bytes 1572872 | tf_op jit(solution)/shard_map/ppermute | solution.py:308
  17.7 3.7 %collective-permute-start.5 = (f32[4,512]{1,0:T(4,128)S(1)}, f32[4,512]{1,0:T(4,128)S(1)}, u32[]{:S(2)}, u32[]{:S(2)}) collective-permute-start(f32[4,512]{1,0:T(4,128)S(1)} %pad_maximum_fusion.refs_5_.refs_3_), channel_id=1, source_target_pairs={{0,1},{1,0},{2,3},{3,2},{4,5},{5,4},{6,7},{7,6},{8,9},{9,8},{10,11... | collective-permute-start | bytes 24584 | tf_op jit(solution)/shard_map/ppermute | solution.py:313
  17.9 3.6 %collective-permute-start.4 = (f32[4,512]{1,0:T(4,128)S(1)}, f32[4,512]{1,0:T(4,128)S(1)}, u32[]{:S(2)}, u32[]{:S(2)}) collective-permute-start(f32[4,512]{1,0:T(4,128)S(1)} %pad_maximum_fusion.refs_5_.refs_3_), channel_id=1, source_target_pairs={{0,16},{16,0},{1,17},{17,1},{2,18},{18,2},{3,19},{19,3},{4,20},{20... | collective-permute-start | bytes 24584 | tf_op jit(solution)/shard_map/ppermute | solution.py:314
  21.4 7.2 %collective-permute-start.6 = (f32[4,512]{1,0:T(4,128)S(1)}, f32[4,512]{1,0:T(4,128)S(1)}, u32[]{:S(2)}, u32[]{:S(2)}) collective-permute-start(f32[4,512]{1,0:T(4,128)S(1)} %collective-permute-done.5.refs_7_.refs_5_), channel_id=1, source_target_pairs={{0,16},{16,0},{1,17},{17,1},{2,18},{18,2},{3,19},{19,3},{4,20},{20... | collective-permute-start | bytes 24584 | tf_op jit(solution)/shard_map/ppermute | solution.py:315
  21.9 21.0 %collective-permute-start.9 = (bf16[256,256]{1,0:T(8,128)(2,1)S(1)}, bf16[256,256]{1,0:T(8,128)(2,1)S(1)}, u32[]{:S(2)}, u32[]{:S(2)}) collective-permute-start(bf16[256,256]{1,0:T(8,128)(2,1)S(1)} %bitcast.10), channel_id=1, source_target_pairs={{0,160},{32,192},{64,224},{96,0},{128,32},{160,64},{192,96},{224,1... | collective-permute-start | bytes 393224 | tf_op jit(solution)/shard_map/ppermute | solution.py:303
  28.6 17.5 %collective-permute-start.8 = (bf16[256,256]{1,0:T(8,128)(2,1)S(1)}, bf16[256,256]{1,0:T(8,128)(2,1)S(1)}, u32[]{:S(2)}, u32[]{:S(2)}) collective-permute-start(bf16[256,256]{1,0:T(8,128)(2,1)S(1)} %bitcast.11), channel_id=1, source_target_pairs={{0,96},{32,128},{64,160},{96,192},{128,224},{160,0},{192,32},{224,... | collective-permute-start | bytes 393224 | tf_op jit(solution)/shard_map/ppermute | solution.py:303
  28.7 17.5 %collective-permute-start.7 = (bf16[256,256]{1,0:T(8,128)(2,1)S(1)}, bf16[256,256]{1,0:T(8,128)(2,1)S(1)}, u32[]{:S(2)}, u32[]{:S(2)}) collective-permute-start(bf16[256,256]{1,0:T(8,128)(2,1)S(1)} %bitcast.12), channel_id=1, source_target_pairs={{0,128},{32,160},{64,192},{96,224},{128,0},{160,32},{192,64},{224,... | collective-permute-start | bytes 393224 | tf_op jit(solution)/shard_map/ppermute | solution.py:303
  42.9 16.5 %collective-permute-start.13 = (bf16[256,256]{1,0:T(8,128)(2,1)S(1)}, bf16[256,256]{1,0:T(8,128)(2,1)S(1)}, u32[]{:S(2)}, u32[]{:S(2)}) collective-permute-start(bf16[256,256]{1,0:T(8,128)(2,1)S(1)} %bitcast.13), channel_id=1, source_target_pairs={{0,224},{32,0},{64,32},{96,64},{128,96},{160,128},{192,160},{224,1... | collective-permute-start | bytes 393224 | tf_op jit(solution)/shard_map/ppermute | solution.py:303
  46.1 13.3 %collective-permute-start.12 = (bf16[256,256]{1,0:T(8,128)(2,1)S(1)}, bf16[256,256]{1,0:T(8,128)(2,1)S(1)}, u32[]{:S(2)}, u32[]{:S(2)}) collective-permute-start(bf16[256,256]{1,0:T(8,128)(2,1)S(1)} %bitcast.14), channel_id=1, source_target_pairs={{0,32},{32,64},{64,96},{96,128},{128,160},{160,192},{192,224},{224... | collective-permute-start | bytes 393224 | tf_op jit(solution)/shard_map/ppermute | solution.py:303
  46.1 13.3 %collective-permute-start.11 = (bf16[256,256]{1,0:T(8,128)(2,1)S(1)}, bf16[256,256]{1,0:T(8,128)(2,1)S(1)}, u32[]{:S(2)}, u32[]{:S(2)}) collective-permute-start(bf16[256,256]{1,0:T(8,128)(2,1)S(1)} %bitcast.15), channel_id=1, source_target_pairs={{0,192},{32,224},{64,0},{96,32},{128,64},{160,96},{192,128},{224,1... | collective-permute-start | bytes 393224 | tf_op jit(solution)/shard_map/ppermute | solution.py:303
  49.0 10.4 %collective-permute-start.10 = (bf16[256,256]{1,0:T(8,128)(2,1)S(1)}, bf16[256,256]{1,0:T(8,128)(2,1)S(1)}, u32[]{:S(2)}, u32[]{:S(2)}) collective-permute-start(bf16[256,256]{1,0:T(8,128)(2,1)S(1)} %bitcast.16), channel_id=1, source_target_pairs={{0,64},{32,96},{64,128},{96,160},{128,192},{160,224},{192,0},{224,... | collective-permute-start | bytes 393224 | tf_op jit(solution)/shard_map/ppermute | solution.py:303
  66.9 9.6 %collective-permute-start.14 = (f32[4,128,512]{2,1,0:T(8,128)S(1)}, f32[4,128,512]{2,1,0:T(8,128)S(1)}, u32[]{:S(2)}, u32[]{:S(2)}) collective-permute-start(f32[4,128,512]{2,1,0:T(8,128)S(1)} %slice.17), channel_id=1, source_target_pairs={{0,16},{16,0},{1,17},{17,1},{2,18},{18,2},{3,19},{19,3},{4,20},{20... | collective-permute-start | bytes 3145736 | tf_op jit(solution)/shard_map/ppermute | solution.py:329
  67.0 11.4 %collective-permute-start.19 = (bf16[256,256]{1,0:T(8,128)(2,1)S(1)}, bf16[256,256]{1,0:T(8,128)(2,1)S(1)}, u32[]{:S(2)}, u32[]{:S(2)}) collective-permute-start(bf16[256,256]{1,0:T(8,128)(2,1)S(1)} %get-tuple-element.29), channel_id=1, source_target_pairs={{0,192},{32,224},{64,0},{96,32},{128,64},{160,96},{192,128},{224,1... | collective-permute-start | bytes 393224 | tf_op jit(solution)/shard_map/ppermute | solution.py:333
  69.1 11.5 %collective-permute-start.20 = (bf16[256,256]{1,0:T(8,128)(2,1)S(1)}, bf16[256,256]{1,0:T(8,128)(2,1)S(1)}, u32[]{:S(2)}, u32[]{:S(2)}) collective-permute-start(bf16[256,256]{1,0:T(8,128)(2,1)S(1)} %get-tuple-element.30), channel_id=1, source_target_pairs={{0,64},{32,96},{64,128},{96,160},{128,192},{160,224},{192,0},{224,... | collective-permute-start | bytes 393224 | tf_op jit(solution)/shard_map/ppermute | solution.py:333
  70.0 21.5 %collective-permute-start.21 = (bf16[256,256]{1,0:T(8,128)(2,1)S(1)}, bf16[256,256]{1,0:T(8,128)(2,1)S(1)}, u32[]{:S(2)}, u32[]{:S(2)}) collective-permute-start(bf16[256,256]{1,0:T(8,128)(2,1)S(1)} %get-tuple-element.31), channel_id=1, source_target_pairs={{0,224},{32,0},{64,32},{96,64},{128,96},{160,128},{192,160},{224,1... | collective-permute-start | bytes 393224 | tf_op jit(solution)/shard_map/ppermute | solution.py:333
  76.5 15.8 %collective-permute-start.16 = (bf16[256,256]{1,0:T(8,128)(2,1)S(1)}, bf16[256,256]{1,0:T(8,128)(2,1)S(1)}, u32[]{:S(2)}, u32[]{:S(2)}) collective-permute-start(bf16[256,256]{1,0:T(8,128)(2,1)S(1)} %get-tuple-element.26), channel_id=1, source_target_pairs={{0,128},{32,160},{64,192},{96,224},{128,0},{160,32},{192,64},{224,... | collective-permute-start | bytes 393224 | tf_op jit(solution)/shard_map/ppermute | solution.py:327
  76.5 17.9 %collective-permute-start.17 = (bf16[256,256]{1,0:T(8,128)(2,1)S(1)}, bf16[256,256]{1,0:T(8,128)(2,1)S(1)}, u32[]{:S(2)}, u32[]{:S(2)}) collective-permute-start(bf16[256,256]{1,0:T(8,128)(2,1)S(1)} %get-tuple-element.27), channel_id=1, source_target_pairs={{0,160},{32,192},{64,224},{96,0},{128,32},{160,64},{192,96},{224,1... | collective-permute-start | bytes 393224 | tf_op jit(solution)/shard_map/ppermute | solution.py:327
  78.4 17.0 %collective-permute-start.18 = (bf16[256,256]{1,0:T(8,128)(2,1)S(1)}, bf16[256,256]{1,0:T(8,128)(2,1)S(1)}, u32[]{:S(2)}, u32[]{:S(2)}) collective-permute-start(bf16[256,256]{1,0:T(8,128)(2,1)S(1)} %get-tuple-element.28), channel_id=1, source_target_pairs={{0,96},{32,128},{64,160},{96,192},{128,224},{160,0},{192,32},{224,... | collective-permute-start | bytes 393224 | tf_op jit(solution)/shard_map/ppermute | solution.py:327
  80.6 17.1 %collective-permute-start.22 = (bf16[256,256]{1,0:T(8,128)(2,1)S(1)}, bf16[256,256]{1,0:T(8,128)(2,1)S(1)}, u32[]{:S(2)}, u32[]{:S(2)}) collective-permute-start(bf16[256,256]{1,0:T(8,128)(2,1)S(1)} %get-tuple-element.32), channel_id=1, source_target_pairs={{0,32},{32,64},{64,96},{96,128},{128,160},{160,192},{192,224},{224... | collective-permute-start | bytes 393224 | tf_op jit(solution)/shard_map/ppermute | solution.py:333
  91.5 20.5 %collective-permute-start.15 = (bf16[4,128,256]{2,1,0:T(8,128)(2,1)S(1)}, bf16[4,128,256]{2,1,0:T(8,128)(2,1)S(1)}, u32[]{:S(2)}, u32[]{:S(2)}) collective-permute-start(bf16[4,128,256]{2,1,0:T(8,128)(2,1)S(1)} %fusion), channel_id=1, source_target_pairs={{0,1},{1,0},{2,3},{3,2},{4,5},{5,4},{6,7},{7,6},{8,9},{9,8},{10,11... | collective-permute-start | bytes 786440 | tf_op jit(solution)/shard_map/ppermute | solution.py:334
